TPU v7x, 8 devices: a whole 2x2x1 slice. The times are simulated.
8 devices in a mesh: rep: 1 (over z), dp: 8 (over x, y, core).
Axes of the slice: x: 2, y: 2, z: 1, core: 2. Of those that a mesh axis runs over, the one named last changes fastest.
Arguments:
- g_w_gate: bfloat16 [8, 2, 1024, 4096], P(('rep', 'dp'))
- g_w_up: bfloat16 [8, 2, 1024, 4096], P(('rep', 'dp'))
- g_w_down: bfloat16 [8, 2, 4096, 1024], P(('rep', 'dp'))
- w_gate: bfloat16 [2, 1024, 4096], replicated
- w_up: bfloat16 [2, 1024, 4096], replicated
- w_down: bfloat16 [2, 4096, 1024], replicated
- m_w_gate: float32 [2, 1024, 4096], P(None, 'dp')
- m_w_up: float32 [2, 1024, 4096], P(None, 'dp')
- m_w_down: float32 [2, 4096, 1024], P(None, 'dp')
- v_w_gate: float32 [2, 1024, 4096], P(None, 'dp')
- v_w_up: float32 [2, 1024, 4096], P(None, 'dp')
- v_w_down: float32 [2, 4096, 1024], P(None, 'dp')
Outputs:
- output 1: bfloat16 [2, 1024, 4096], P('rep')
- output 2: bfloat16 [2, 1024, 4096], P('rep')
- output 3: bfloat16 [2, 4096, 1024], P('rep')
- output 4: float32 [2, 1024, 4096], P('rep', 'dp')
- output 5: float32 [2, 1024, 4096], P('rep', 'dp')
- output 6: float32 [2, 4096, 1024], P('rep', 'dp')
- output 7: float32 [2, 1024, 4096], P('rep', 'dp')
- output 8: float32 [2, 1024, 4096], P('rep', 'dp')
- output 9: float32 [2, 4096, 1024], P('rep', 'dp')
All inputs are finite; a program needn't handle non-finite values.
Results may differ from a plain program's by a relative error of at most 0.022.
Values are sent between devices in bfloat16 or wider.
A program may use at most 2 GiB of HBM per device.

v0:
```python
import jax
import jax.numpy as jnp
from jax import lax
from jax.sharding import PartitionSpec as P


def adamw(w, m, v, g):
    m = 0.9 * m + 0.1 * g
    v = 0.95 * v + 0.05 * g * g
    step = m * lax.rsqrt(v + 1e-8) + 0.1 * w
    return (w - 0.02 * step).astype(jnp.bfloat16), m, v


def clipped(gradients, sum_of_squares, count):
    factor = jnp.minimum(1.0, 0.5 * lax.rsqrt(sum_of_squares / count + 1e-30))
    return [g * factor for g in gradients]


def solution(mesh):
    def step(*arrays):
        terms, weights, m, v = (arrays[i : i + 3] for i in (0, 3, 6, 9))
        gradients = [lax.psum_scatter(t[0], "dp", scatter_dimension=1, tiled=True).astype(jnp.float32) for t in terms]
        squares = lax.psum(sum(jnp.sum(g * g) for g in gradients), "dp")
        gradients = clipped(gradients, squares, lax.psum(1, "dp") * sum(g.size for g in gradients))
        me = lax.axis_index("dp")
        own = [lax.dynamic_slice_in_dim(w, me * one.shape[1], one.shape[1], 1).astype(jnp.float32) for w, one in zip(weights, m, strict=True)]
        new = [adamw(w, m, v, g) for w, m, v, g in zip(own, m, v, gradients, strict=True)]
        whole = [lax.all_gather(one[0], "dp", axis=1, tiled=True) for one in new]
        return (*whole, *(one[1] for one in new), *(one[2] for one in new))

    all_of, cut = P(None, None, None), P(None, "dp", None)
    return jax.shard_map(
        step,
        mesh=mesh,
        in_specs=(P(("rep", "dp"), None, None, None),) * 3 + (all_of,) * 3 + (cut,) * 6,
        out_specs=(P("rep", None, None),) * 3 + (P("rep", "dp", None),) * 6,
        check_vma=False,
    )
```

profile of v0, /device:TPU:0, one launch (start us, length us, event | category | flops | bytes accessed | tf_op | source)
XLA Modules:
  0.0 677.1 jit_solution(14795979777214780134)
XLA Ops:
  7.2 0.0 reduce-scatter.4.cloned.1.call-start
  7.2 0.7 reduce-scatter.4.cloned.1.call-update
  7.9 0.0 reduce-scatter.6.cloned.1.call-start
  8.0 0.7 reduce-scatter.6.cloned.1.call-update
  8.7 0.0 reduce-scatter.8.cloned.1.call-start
  8.7 0.7 reduce-scatter.8.cloned.1.call-update
  9.4 0.0 all-gather.8.cloned.1.call-start
  9.4 111.8 %reduce-scatter.4.cloned.1.call-done = bf16[2,128,4096]{2,1,0:T(8,128)(2,1)} async-done(((bf16[2,1024,4096]{2,1,0:T(8,128)(2,1)}), bf16[2,128,4096]{2,1,0:T(8,128)(2,1)}) %reduce-scatter.4.cloned.1.call-update) | async-done | bytes 2097168 | tf_op jit(solution)/shard_map/reduce_scatter | solution.py:22
  121.3 3.3 fusion.9
  124.6 107.2 %reduce-scatter.6.cloned.1.call-done = bf16[2,128,4096]{2,1,0:T(8,128)(2,1)} async-done(((bf16[2,1024,4096]{2,1,0:T(8,128)(2,1)}), bf16[2,128,4096]{2,1,0:T(8,128)(2,1)}) %reduce-scatter.6.cloned.1.call-update) | async-done | bytes 2097168 | tf_op jit(solution)/shard_map/reduce_scatter | solution.py:22
  231.8 3.3 fusion.10
  236.3 105.9 %reduce-scatter.8.cloned.1.call-done = bf16[2,512,1024]{2,1,0:T(8,128)(2,1)} async-done(((bf16[2,4096,1024]{2,1,0:T(8,128)(2,1)}), bf16[2,512,1024]{2,1,0:T(8,128)(2,1)}) %reduce-scatter.8.cloned.1.call-update) | async-done | bytes 2097168 | tf_op jit(solution)/shard_map/reduce_scatter | solution.py:22
  342.2 3.3 fusion.11
  346.2 22.3 %psum.7 = f32[]{:T(128)} all-reduce(f32[]{:T(128)S(6)} %add.65), channel_id=1, replica_groups=mesh['rep'=1,'dp'=8] {'dp'}, use_global_device_ids=true, to_apply=%region_6.0 | all-reduce | flops 1 | bytes 8 | tf_op jit(solution)/shard_map/psum | solution.py:23
  369.1 8.2 %fusion.17 = (bf16[2,512,1024]{2,1,0:T(8,128)(2,1)}, f32[2,512,1024]{2,1,0:T(8,128)}, f32[2,512,1024]{2,1,0:T(8,128)}) fusion(bf16[2,4096,1024]{2,1,0:T(8,128)(2,1)} %param.17, s32[]{:T(128)S(6)} %select_n.8, f32[]{:T(128)S(6)} %min_shard_map.3, bf16[2,512,1024]{2,1,0:T(8,128)(2,1)} %reduce-scatter.8.cloned.1.call-done, f32[2,512,1024]{2,1,0:T(8,128)} %param.23, ...), kind=kLoop, calls=%fused_computation.32 | loop fusion | flops 17825792 | bytes 23068680 | tf_op jit(solution)/shard_map/convert_element_type | solution.py:11
  377.3 0.0 all-gather.8.cloned.1.call-update
  377.3 0.0 all-gather.4.cloned.1.call-start
  377.3 0.0 copy-start.1
  377.4 8.4 %fusion.8 = (bf16[2,128,4096]{2,1,0:T(8,128)(2,1)}, f32[2,128,4096]{2,1,0:T(8,128)}, f32[2,128,4096]{2,1,0:T(8,128)}) fusion(bf16[2,1024,4096]{2,1,0:T(8,128)(2,1)} %param.15, s32[]{:T(128)S(6)} %select_n.7, f32[]{:T(128)S(6)} %min_shard_map.3, bf16[2,128,4096]{2,1,0:T(8,128)(2,1)} %reduce-scatter.4.cloned.1.call-done, f32[2,128,4096]{2,1,0:T(8,128)} %param.21, ...), kind=kLoop, calls=%fused_computation.23 | loop fusion | flops 17825792 | bytes 23068680 | tf_op jit(solution)/shard_map/convert_element_type | solution.py:11
  385.8 0.0 all-gather.4.cloned.1.call-update
  385.8 0.0 all-gather.6.cloned.1.call-start
  385.9 0.0 copy-done.1
  385.9 7.1 %fusion.14 = (bf16[2,128,4096]{2,1,0:T(8,128)(2,1)}, f32[2,128,4096]{2,1,0:T(8,128)}, f32[2,128,4096]{2,1,0:T(8,128)}) fusion(bf16[2,1024,4096]{2,1,0:T(8,128)(2,1)} %param.16, s32[]{:T(128)S(6)} %select_n.7, f32[]{:T(128)S(6)} %min_shard_map.3, bf16[2,128,4096]{2,1,0:T(8,128)(2,1)S(1)} %copy-done.1, f32[2,128,4096]{2,1,0:T(8,128)} %param.22, ...), kind=kLoop, calls=%fused_computation.29 | loop fusion | flops 17825792 | bytes 23068680 | tf_op jit(solution)/shard_map/convert_element_type | solution.py:11
  393.0 0.0 all-gather.6.cloned.1.call-update
  393.0 70.4 %all-gather.8.cloned.1.call-done = bf16[2,4096,1024]{2,1,0:T(8,128)(2,1)} async-done(((bf16[2,512,1024]{2,1,0:T(8,128)(2,1)}), bf16[2,4096,1024]{2,1,0:T(8,128)(2,1)}) %all-gather.8.cloned.1.call-update) | async-done | bytes 16777232 | tf_op jit(solution)/shard_map/all_gather | solution.py:28
  463.4 86.4 %all-gather.4.cloned.1.call-done = bf16[2,1024,4096]{2,1,0:T(8,128)(2,1)} async-done(((bf16[2,128,4096]{2,1,0:T(8,128)(2,1)}), bf16[2,1024,4096]{2,1,0:T(8,128)(2,1)}) %all-gather.4.cloned.1.call-update) | async-done | bytes 16777232 | tf_op jit(solution)/shard_map/all_gather | solution.py:28
  549.8 86.4 %all-gather.6.cloned.1.call-done = bf16[2,1024,4096]{2,1,0:T(8,128)(2,1)} async-done(((bf16[2,128,4096]{2,1,0:T(8,128)(2,1)}), bf16[2,1024,4096]{2,1,0:T(8,128)(2,1)}) %all-gather.6.cloned.1.call-update) | async-done | bytes 16777232 | tf_op jit(solution)/shard_map/all_gather | solution.py:28
  636.2 0.0 copy-start
  636.2 0.0 slice-start
  636.2 0.0 slice-start.1
  636.2 16.8 %copy.24 = bf16[2,1024,4096]{2,1,0:T(8,128)(2,1)} copy(bf16[2,1024,4096]{2,1,0:T(8,128)(2,1)} %all-gather.4.cloned.1.call-done) | data formatting | bytes 33554432
  652.9 0.0 copy-done
  653.0 0.0 slice-start.2
  653.0 0.0 slice-start.3
  653.0 8.5 %copy.25 = bf16[2,1024,4096]{2,1,0:T(8,128)(2,1)} copy(bf16[2,1024,4096]{2,1,0:T(8,128)(2,1)S(1)} %copy-done) | data formatting | bytes 33554432
  661.5 0.0 slice-done
  661.5 0.0 slice-done.1
  661.5 1.4 slice-done.2
  662.9 1.2 slice-done.3
  664.1 6.2 copy.26
  (1 shorter events, 0.0 us)
Async XLA Ops:
  7.2 114.1 %reduce-scatter.4.cloned.1.call-start = ((), (), s32[]{:S(2)}) async-start(), calls=%async_computation.3 | async-start | bytes 18874368 | tf_op jit(solution)/shard_map/reduce_scatter | solution.py:22
  7.9 223.8 %reduce-scatter.6.cloned.1.call-start = ((), (), s32[]{:S(2)}) async-start(), calls=%async_computation.4 | async-start | bytes 18874368 | tf_op jit(solution)/shard_map/reduce_scatter | solution.py:22
  8.7 333.6 %reduce-scatter.8.cloned.1.call-start = ((), (), s32[]{:S(2)}) async-start(), calls=%async_computation.5 | async-start | bytes 18874368 | tf_op jit(solution)/shard_map/reduce_scatter | solution.py:22
  9.4 454.0 %all-gather.8.cloned.1.call-start = ((), (), s32[]{:S(2)}) async-start(), calls=%async_computation.8 | async-start | bytes 18874368 | tf_op jit(solution)/shard_map/all_gather | solution.py:28
  377.3 172.5 %all-gather.4.cloned.1.call-start = ((), (), s32[]{:S(2)}) async-start(), calls=%async_computation.6 | async-start | bytes 18874368 | tf_op jit(solution)/shard_map/all_gather | solution.py:28
  377.3 8.5 %copy-start.1 = (bf16[2,128,4096]{2,1,0:T(8,128)(2,1)S(1)}, bf16[2,128,4096]{2,1,0:T(8,128)(2,1)}, u32[]{:S(2)}) copy-start(bf16[2,128,4096]{2,1,0:T(8,128)(2,1)} %reduce-scatter.6.cloned.1.call-done) | copy-start | bytes 6291460
  385.8 250.3 %all-gather.6.cloned.1.call-start = ((), (), s32[]{:S(2)}) async-start(), calls=%async_computation.7 | async-start | bytes 18874368 | tf_op jit(solution)/shard_map/all_gather | solution.py:28
  636.2 16.8 %copy-start = (bf16[2,1024,4096]{2,1,0:T(8,128)(2,1)S(1)}, bf16[2,1024,4096]{2,1,0:T(8,128)(2,1)}, u32[]{:S(2)}) copy-start(bf16[2,1024,4096]{2,1,0:T(8,128)(2,1)} %all-gather.6.cloned.1.call-done) | copy-start | bytes 50331652
  636.2 25.3 %slice-start = ((s8[16777216]{0:T(1024)(128)(4,1)}), s8[4194304]{0:T(1024)(128)(4,1)S(1)}, s32[]{:S(2)}) async-start(s8[16777216]{0:T(1024)(128)(4,1)} %bitcast.6), calls=%async_computation.9 | async-start | bytes 8388608
  636.2 25.3 %slice-start.1 = ((s8[16777216]{0:T(1024)(128)(4,1)}), s8[4194304]{0:T(1024)(128)(4,1)S(1)}, s32[]{:S(2)}) async-start(s8[16777216]{0:T(1024)(128)(4,1)} %bitcast.6), calls=%async_computation.10 | async-start | bytes 8388608
  653.0 9.9 %slice-start.2 = ((s8[16777216]{0:T(1024)(128)(4,1)}), s8[4194304]{0:T(1024)(128)(4,1)S(1)}, s32[]{:S(2)}) async-start(s8[16777216]{0:T(1024)(128)(4,1)} %bitcast.6), calls=%async_computation.11 | async-start | bytes 8388608
  653.0 11.1 %slice-start.3 = ((s8[16777216]{0:T(1024)(128)(4,1)}), s8[4194304]{0:T(1024)(128)(4,1)S(1)}, s32[]{:S(2)}) async-start(s8[16777216]{0:T(1024)(128)(4,1)} %bitcast.6), calls=%async_computation.12 | async-start | bytes 8388608
Sparse Core Ops, SparseCore 0:
  11.5 109.7 reduce-scatter.3
  124.8 106.9 reduce-scatter.5
  235.3 106.9 reduce-scatter.7
  377.4 85.9 all-gather.7
  465.7 84.0 all-gather.3
  552.0 84.0 all-gather.5
where the time goes:
time: 677 us
  waiting for transfers between devices  570 us (84%)
  local copies, waits for them, and re-layouts  34.1 us (5%)
  other arithmetic  33.5 us (5%)
  blocking collectives  22.3 us (3%)
  between operations  16.8 us (2%)
    reduce_scatter x3, waiting for transfers between devices, step(): lax.psum_scatter(t[0], 'dp', scatter_dimension=1, tiled=True)  325 us
    all_gather x3, waiting for transfers between devices, step(): whole = [lax.all_gather(one[0], 'dp', axis=1, tiled=True) for one in new]  243 us
    unnamed x15, local copies, waits for them, and re-layouts  34.1 us
    convert_element_type x3, other arithmetic, adamw(): return ((w - 0.02 * step).astype(jnp.bfloat16), m, v)  23.7 us
    psum x1, blocking collectives, step(): squares = lax.psum(sum((jnp.sum(g * g) for g in gradients)), 'dp')  22.3 us
  transfers between devices with their start and end apart: 6, of which 6 were waited for; matrix products, arithmetic and copies ran while one was open for 3% of the time, Pallas kernels for 0%

commit v1 on v0

v1 whole, which is shorter than its diff:
```python
import functools

import jax
import jax.numpy as jnp
from jax import lax
from jax.experimental import pallas as pl
from jax.experimental.pallas import tpu as pltpu
from jax.sharding import PartitionSpec as P

BF, F32 = jnp.bfloat16, jnp.float32
RING = 4
FEED = 2
ME, XN, YN, DG = range(4)
XD, XO, XT, YD, YO, YT = range(6)


def moments(m, v, g):
    return 0.9 * m + 0.1 * g, 0.95 * v + 0.05 * g * g


def kernel(*refs, n, layers, count):
    it = iter(refs)
    take = lambda k: [next(it) for _ in range(k)]
    g, w, m, v = take(3), take(3), take(3), take(3)
    whole, gsum, factor_ref = take(3), take(3), next(it)
    pair, land = take(3), take(3)
    gring, mring, vring, wring = take(2), take(2), take(2), take(2)
    squares, factor_v = take(2)
    d2d_s, d2d_r, lk_s, lk_r, ring_s, feed_s = take(6)
    sq_s, sq_r, own_s, own_r, fwd_s, fwd_r, rel_s, rel_r, loc_s = take(9)

    me = lax.axis_index("dp")
    core, chip = me % 2, me // 2
    cy, cx = chip % 2, chip // 2
    at = lambda x, y, c: 4 * x + 2 * y + c
    mate = at(cx, cy, 1 - core)
    xnbr, ynbr = at(1 - cx, cy, core), at(cx, 1 - cy, core)
    owners = [lambda c: at(cx, cy, c), lambda c: at(1 - cx, cy, c), lambda c: at(cx, 1 - cy, c), lambda c: at(1 - cx, 1 - cy, c)]

    def remote(src, dst, s, r, device):
        return pltpu.make_async_remote_copy(
            src_ref=src, dst_ref=dst, send_sem=s, recv_sem=r, device_id={"dp": device}, device_id_type=pl.DeviceIdType.MESH
        )

    barrier = pltpu.get_barrier_semaphore()
    for k in range(1, n):
        pl.semaphore_signal(barrier, inc=1, device_id={"dp": (me + k) % n}, device_id_type=pl.DeviceIdType.MESH)
    pl.semaphore_wait(barrier, n - 1)

    units = [(i, layer) for i in range(3) for layer in range(layers)]
    kind = [0, 0, 1]
    half = [pair[i].shape[3] for i in range(3)]

    def rows(i, device, h):
        return pl.ds(pl.multiple_of(device * (2 * half[i]) + h * half[i], half[i]), half[i])

    steps = []
    for u in range(len(units)):
        steps += [("send", DG, u, 0, XD, None), ("send", DG, u, 1, YD, None)]
    for u in range(len(units)):
        steps += [("send", XN, u, 0, XO, None), ("send", YN, u, 1, YO, None)]
    for u in range(len(units)):
        steps += [("send", YN, u, 0, YT, XD), ("send", XN, u, 1, XT, YD)]
    for u in range(len(units)):
        steps += [("sum", ME, u, 0, XO, YT), ("sum", ME, u, 1, YO, XT)]

    def exchange(step):
        _, block, u, h, _, _ = step
        i, layer = units[u]
        return remote(
            g[i].at[0, layer, rows(i, owners[block](1 - core), h)], pair[i].at[block, layer, h], d2d_s.at[block, u, h], d2d_r.at[block, u, h], mate
        )

    order = {0: [], 1: []}
    for k, step in enumerate(steps):
        order[kind[units[step[2]][0]]].append(k)
    place = {k: (c, p) for c in order for p, k in enumerate(order[c])}

    def term(k):
        _, block, u, h, _, _ = steps[k]
        i, layer = units[u]
        c, p = place[k]
        slot = p % RING
        return pltpu.make_async_copy(g[i].at[0, layer, rows(i, owners[block](core), h)], gring[c].at[slot], ring_s.at[c, slot])

    def push(step):
        _, block, u, h, stream, _ = step
        i, layer = units[u]
        return remote(pair[i].at[block, layer, h], land[i].at[stream, layer], lk_s.at[stream, u], lk_r.at[stream, u], xnbr if stream < YD else ynbr)

    def arrived(stream, u):
        i, layer = units[u]
        return remote(land[i].at[stream, layer], land[i].at[stream, layer], lk_s.at[stream, u], lk_r.at[stream, u], xnbr if stream < YD else ynbr)

    ahead = 12
    exchanged, started = 0, {0: 0, 1: 0}

    def next_exchange():
        nonlocal exchanged
        if exchanged < len(steps):
            exchange(steps[exchanged]).start()
            exchanged += 1

    def next_term(c):
        if started[c] < len(order[c]):
            term(order[c][started[c]]).start()
            started[c] += 1

    next_exchange()
    next_exchange()
    for _ in range(RING):
        next_term(0)
    for _ in range(ahead - 2):
        next_exchange()
    for _ in range(RING):
        next_term(1)

    def feed(u, h, k):
        i, layer = units[u]
        c, slot = kind[i], k % FEED
        mine = pl.ds(h * half[i], half[i])
        return [
            pltpu.make_async_copy(m[i].at[layer, mine], mring[c].at[slot], feed_s.at[0, c, slot]),
            pltpu.make_async_copy(v[i].at[layer, mine], vring[c].at[slot], feed_s.at[1, c, slot]),
            pltpu.make_async_copy(w[i].at[layer, rows(i, me, h)], wring[c].at[slot], feed_s.at[2, c, slot]),
        ]

    fed = [(u, h) for u in range(len(units)) for h in range(2)]
    feed_order = {c: [k for k, (u, h) in enumerate(fed) if kind[units[u][0]] == c] for c in (0, 1)}
    feed_at = {k: p for c in (0, 1) for p, k in enumerate(feed_order[c])}
    for c in (0, 1):
        for k in feed_order[c][:FEED]:
            for copy in feed(*fed[k], feed_at[k]):
                copy.start()

    zero = jnp.zeros((8, 128), F32)
    total = (zero,) * 4
    for k, step in enumerate(steps):
        what, block, u, h, stream, other = step
        i, layer = units[u]
        c, p = place[k]
        exchange_in = remote(pair[i].at[block, layer, h], pair[i].at[block, layer, h], d2d_s.at[block, u, h], d2d_r.at[block, u, h], mate)
        exchange_in.wait_recv()
        term(k).wait()
        more = []
        if what == "sum":
            arrived(stream, u).wait_recv()
            more.append(land[i].at[stream, layer])
        if other is not None:
            arrived(other, u).wait_recv()
            more.append(land[i].at[other, layer])
        dst, own = pair[i].at[block, layer, h], gring[c].at[p % RING]
        cols = dst.shape[1]
        tile = 65536 // cols

        def body(r, acc, dst=dst, own=own, more=more, cols=cols, tile=tile, what=what):
            at_rows = pl.ds(pl.multiple_of(r * tile, tile), tile)
            s = own[at_rows, :].astype(F32) + dst[at_rows, :].astype(F32)
            for one in more:
                s = s + one[at_rows, :].astype(F32)
            b = s.astype(BF)
            dst[at_rows, :] = b
            if what == "sum":
                q = b.astype(F32)
                q = q * q
                acc = list(acc)
                for a in range(tile // 8):
                    for z in range(cols // 128):
                        acc[(a + z) % 4] = acc[(a + z) % 4] + q[8 * a : 8 * a + 8, 128 * z : 128 * z + 128]
                acc = tuple(acc)
            return acc

        done = lax.fori_loop(0, half[i] // tile, body, total if what == "sum" else ())
        total = done if what == "sum" else total
        next_term(c)
        next_exchange()
        if what == "send":
            push(step).start()
        else:
            pltpu.make_async_copy(dst, gsum[i].at[layer, pl.ds(h * half[i], half[i])], loc_s.at[0, u, h]).start()

    squares[n] = total[0] + total[1] + total[2] + total[3]
    for k in range(1, n):
        remote(squares.at[n], squares.at[me], sq_s.at[k], sq_r.at[me], (me + k) % n).start()
    for step in steps:
        exchange(step).wait_send()
        if step[0] == "send":
            push(step).wait_send()
    squares[me] = squares[n]
    for k in range(1, n):
        remote(squares.at[n], squares.at[(me + k) % n], sq_s.at[k], sq_r.at[(me + k) % n], (me + k) % n).wait_recv()
    everything = squares[0]
    for k in range(1, n):
        everything = everything + squares[k]
    everything = jnp.sum(jnp.sum(everything, axis=0, keepdims=True), axis=1, keepdims=True)
    factor = jnp.minimum(1.0, 0.5 * lax.rsqrt(everything / count + 1e-30))
    factor_v[...] = jnp.broadcast_to(factor, (8, 128))

    def out(i, layer, device, h):
        return whole[i].at[layer, rows(i, device, h)]

    def own_copies(u, h):
        i, layer = units[u]
        src = pair[i].at[DG, layer, h]
        dst = out(i, layer, me, h)
        return [
            functools.partial(remote, src, dst, own_s.at[0, u, h], own_r.at[0, u, h], xnbr),
            functools.partial(remote, src, dst, own_s.at[1, u, h], own_r.at[1, u, h], ynbr),
            functools.partial(remote, src, dst, rel_s.at[ME, u, h], rel_r.at[ME, u, h], mate),
            functools.partial(pltpu.make_async_copy, src, dst, loc_s.at[1, u, h]),
        ]

    for k, (u, h) in enumerate(fed):
        i, layer = units[u]
        c, slot = kind[i], feed_at[k] % FEED
        for copy in feed(u, h, feed_at[k]):
            copy.wait()
        dst, src, mm, vv, ww = pair[i].at[DG, layer, h], pair[i].at[ME, layer, h], mring[c].at[slot], vring[c].at[slot], wring[c].at[slot]
        cols = dst.shape[1]
        tile = 32768 // cols if cols < 4096 else 16

        def body(r, _, dst=dst, src=src, mm=mm, vv=vv, ww=ww, tile=tile):
            at_rows = pl.ds(pl.multiple_of(r * tile, tile), tile)
            grad = src[at_rows, :].astype(F32) * factor_v[0:1, 0:1]
            m_new, v_new = moments(mm[at_rows, :], vv[at_rows, :], grad)
            weight = ww[at_rows, :].astype(F32)
            dst[at_rows, :] = (weight - 0.02 * (m_new * lax.rsqrt(v_new + 1e-8) + 0.1 * weight)).astype(BF)
            return 0

        lax.fori_loop(0, half[i] // tile, body, 0)
        if feed_at[k] + FEED < len(feed_order[c]):
            later = feed_order[c][feed_at[k] + FEED]
            for copy in feed(*fed[later], feed_at[later]):
                copy.start()
        for copy in own_copies(u, h):
            copy().start()

    started_late = []

    def relay(u, h, block):
        i, layer = units[u]
        here = out(i, layer, owners[block](core), h)
        copy = remote(here, here, rel_s.at[block, u, h], rel_r.at[block, u, h], mate)
        copy.start()
        started_late.append(copy)

    def onward(u, h, block, to, device):
        i, layer = units[u]
        here = out(i, layer, owners[block](core), h)
        copy = remote(here, here, fwd_s.at[to, u], fwd_r.at[to, u], device)
        copy.start()
        started_late.append(copy)

    def from_link(u, h, which):
        i, layer = units[u]
        there = out(i, layer, owners[(XN, YN)[which]](core), h)
        remote(there, there, own_s.at[which, u, h], own_r.at[which, u, h], (xnbr, ynbr)[which]).wait_recv()

    for u in range(len(units)):
        from_link(u, 0, 0)
        onward(u, 0, XN, 1, ynbr)
        relay(u, 0, XN)
        from_link(u, 0, 1)
        relay(u, 0, YN)
        from_link(u, 1, 1)
        onward(u, 1, YN, 0, xnbr)
        relay(u, 1, YN)
        from_link(u, 1, 0)
        relay(u, 1, XN)
    for u in range(len(units)):
        i, layer = units[u]
        for h, to, device in ((0, 1, ynbr), (1, 0, xnbr)):
            there = out(i, layer, owners[DG](core), h)
            remote(there, there, fwd_s.at[to, u], fwd_r.at[to, u], device).wait_recv()
            relay(u, h, DG)

    for copy in started_late:
        copy.wait_send()
    for u, h in fed:
        i, layer = units[u]
        for copy in own_copies(u, h)[:3]:
            copy().wait_send()
        own_copies(u, h)[3]().wait()
        pltpu.make_async_copy(pair[i].at[ME, layer, h], gsum[i].at[layer, pl.ds(h * half[i], half[i])], loc_s.at[0, u, h]).wait()
        for block in range(4):
            there = out(i, layer, owners[block](1 - core), h)
            remote(there, there, rel_s.at[block, u, h], rel_r.at[block, u, h], mate).wait_recv()
    for k in range(1, n):
        remote(squares.at[n], squares.at[me], sq_s.at[k], sq_r.at[me], (me + k) % n).wait_send()
    done = pltpu.make_async_copy(factor_v, factor_ref, loc_s.at[0, 0, 0])
    done.start()
    done.wait()


def solution(mesh):
    n = mesh.shape["dp"]

    def step(*arrays):
        terms, weights, m, v = (arrays[i : i + 3] for i in (0, 3, 6, 9))
        layers = weights[0].shape[0]
        blocks = [(one.shape[1] // 2, one.shape[2]) for one in m]
        kinds = (blocks[0], blocks[2])
        count = float(n * sum(one.size for one in m))
        dma = pltpu.SemaphoreType.DMA
        units = 3 * layers
        any_space = pl.BlockSpec(memory_space=pl.ANY)
        out = pl.pallas_call(
            functools.partial(kernel, n=n, layers=layers, count=count),
            name="step",
            out_shape=[jax.ShapeDtypeStruct(one.shape, BF) for one in weights]
            + [jax.ShapeDtypeStruct(one.shape, BF) for one in m]
            + [jax.ShapeDtypeStruct((8, 128), F32)],
            in_specs=[any_space] * 12,
            out_specs=[any_space] * 7,
            scratch_shapes=[pltpu.VMEM((4, layers, 2, *b), BF) for b in blocks]
            + [pltpu.VMEM((6, layers, *b), BF) for b in blocks]
            + [pltpu.VMEM((RING, *b), BF) for b in kinds]
            + [pltpu.VMEM((FEED, *b), F32) for b in kinds] * 2
            + [pltpu.VMEM((FEED, *b), BF) for b in kinds]
            + [pltpu.VMEM((n + 1, 8, 128), F32), pltpu.VMEM((8, 128), F32)]
            + [dma((4, units, 2)), dma((4, units, 2)), dma((6, units)), dma((6, units)), dma((2, RING)), dma((3, 2, FEED))]
            + [dma((n,)), dma((n,)), dma((2, units, 2)), dma((2, units, 2)), dma((2, units)), dma((2, units))]
            + [dma((4, units, 2)), dma((4, units, 2)), dma((2, units, 2))],
            compiler_params=pltpu.CompilerParams(collective_id=0, has_side_effects=True, vmem_limit_bytes=62 * 2**20),
        )(*terms, *weights, *m, *v)
        whole, sums, factor = out[:3], out[3:6], out[6][0, 0]
        new = [moments(a, b, s.astype(F32) * factor) for a, b, s in zip(m, v, sums, strict=True)]
        return (*whole, *(one[0] for one in new), *(one[1] for one in new))

    all_of, cut = P(None, None, None), P(None, "dp", None)
    return jax.shard_map(
        step,
        mesh=mesh,
        in_specs=(P(("rep", "dp"), None, None, None),) * 3 + (all_of,) * 3 + (cut,) * 6,
        out_specs=(P("rep", None, None),) * 3 + (P("rep", "dp", None),) * 6,
        check_vma=False,
    )
```

time: 677 us -> 483 us (0.71)
  waiting for transfers between devices: 570 us -> 0 us
  Pallas kernels: 0 us -> 426 us
  blocking collectives: 22.3 us -> 0 us
  between operations: 16.8 us -> 0.74 us
  other arithmetic: 33.5 us -> 21.3 us
    pallas_call x0 -> x1, Pallas kernels: none -> 426 us  [step(): pl.pallas_call(functools.partial(kernel, n=n, layers=layers, count=count)...]
    reduce_scatter x3 -> x0, waiting for transfers between devices: 325 us -> none  [step(): lax.psum_scatter(t[0], 'dp', scatter_dimension=1, tiled=True)]
    all_gather x3 -> x0, waiting for transfers between devices: 243 us -> none  [step(): whole = [lax.all_gather(one[0], 'dp', axis=1, tiled=True) for one in new]]
    convert_element_type x3 -> x0, other arithmetic: 23.7 us -> none  [adamw(): return ((w - 0.02 * step).astype(jnp.bfloat16), m, v)]
    psum x1 -> x0, blocking collectives: 22.3 us -> none  [step(): squares = lax.psum(sum((jnp.sum(g * g) for g in gradients)), 'dp')]
    add x0 -> x2, other arithmetic: none -> 21.3 us  [moments(): return (0.9 * m + 0.1 * g, 0.95 * v + 0.05 * g * g)]
    reduce_sum x3 -> x0, other arithmetic: 9.82 us -> none  [step(): squares = lax.psum(sum((jnp.sum(g * g) for g in gradients)), 'dp')]
    unnamed x15 -> x25, local copies, waits for them, and re-layouts: 34.1 us -> 32.6 us
  transfers between devices with their start and end apart: 6 -> 0, of which waited for: 6 -> 0; matrix products, arithmetic and copies ran while one was open for 3% -> 0% of each run, Pallas kernels for 0% -> 0%
where the time goes in v1:
time: 483 us; the launch traced here: 482 us
  Pallas kernels  426 us (88%)
  local copies, waits for them, and re-layouts  33.8 us (7%)
  other arithmetic  21.3 us (4%)
    pallas_call x1, Pallas kernels, step(): pl.pallas_call(functools.partial(kernel, n=n, layers=layers, count=count)...  426 us
    unnamed x25, local copies, waits for them, and re-layouts  32.6 us
    add x2, other arithmetic, moments(): return (0.9 * m + 0.1 * g, 0.95 * v + 0.05 * g * g)  21.3 us

profile of v1, /device:TPU:0, one launch (start us, length us, event | category | flops | bytes accessed | tf_op | source)
XLA Modules:
  0.0 482.2 jit_solution(7596241936349565668)
XLA Ops:
  0.6 426.3 %step.1 = (bf16[2,1024,4096]{2,1,0:T(8,128)(2,1)}, bf16[2,1024,4096]{2,1,0:T(8,128)(2,1)}, bf16[2,4096,1024]{2,1,0:T(8,128)(2,1)}, bf16[2,128,4096]{2,1,0:T(8,12...) custom-call(bf16[1,2,1024,4096]{3,2,1,0:T(8,128)(2,1)} %refs_0_.1, ...), custom_call_target="tpu_custom_call" | custom-call | tf_op jit(solution)/shard_map/step/pallas_call | solution.py:307
  427.0 1.2 slice.3
  428.2 0.0 copy-start
  428.2 0.0 copy-start.1
  428.2 0.0 copy-start.2
  428.2 15.7 %fusion = (f32[2,128,4096]{2,1,0:T(8,128)}, f32[2,128,4096]{2,1,0:T(8,128)}, f32[2,128,4096]{2,1,0:T(8,128)}, f32[2,128,4096]{2,1,0:T(8,128)}) fusion(f32[2,128,4096]{2,1,0:T(8,128)} %refs_9_.1, bf16[2,128,4096]{2,1,0:T(8,128)(2,1)} %get-tuple-element.19, f32[]{:T(128)} %bitcast, f32[2,128,4096]{2,1,0:T(8,128)} %refs_6_.1, ...), kind=kLoop, calls=%fused_computation.3 | loop fusion | flops 18874368 | bytes 37748740 | tf_op jit(solution)/shard_map/add | solution.py:18
  443.9 0.0 copy-done
  443.9 0.0 copy-done.1
  443.9 0.0 copy-done.2
  443.9 0.0 slice-start.4
  443.9 0.0 slice-start.5
  443.9 5.6 %fusion.2 = (f32[2,512,1024]{2,1,0:T(8,128)}, f32[2,512,1024]{2,1,0:T(8,128)}) fusion(f32[2,512,1024]{2,1,0:T(8,128)S(1)} %copy-done.1, bf16[2,512,1024]{2,1,0:T(8,128)(2,1)S(1)} %copy-done.2, f32[]{:T(128)} %bitcast, f32[2,512,1024]{2,1,0:T(8,128)S(1)} %copy-done), kind=kLoop, calls=%fused_computation.5 | loop fusion | flops 9437184 | bytes 18874372 | tf_op jit(solution)/shard_map/add | solution.py:18
  449.6 0.0 slice-start.6
  449.6 0.0 slice-start.7
  449.6 0.0 slice-start
  449.6 0.0 slice-start.1
  449.6 17.0 %copy.24 = bf16[2,1024,4096]{2,1,0:T(8,128)(2,1)} copy(bf16[2,1024,4096]{2,1,0:T(8,128)(2,1)} %get-tuple-element.40) | data formatting | bytes 33554432
  466.5 0.0 slice-done.4
  466.5 0.0 slice-done.5
  466.5 0.0 slice-done.6
  466.5 0.0 slice-done.7
  466.6 0.0 slice-start.2
  466.6 0.0 slice-start.3
  466.6 8.5 %copy.25 = bf16[2,1024,4096]{2,1,0:T(8,128)(2,1)} copy(bf16[2,1024,4096]{2,1,0:T(8,128)(2,1)S(1)} %bitcast.4) | data formatting | bytes 33554432
  475.1 0.0 slice-done
  475.1 0.0 slice-done.1
  475.1 0.0 slice-done.2
  475.1 1.0 slice-done.3
  476.1 6.2 %copy.26 = bf16[2,4096,1024]{2,1,0:T(8,128)(2,1)} copy(bf16[2,4096,1024]{2,1,0:T(8,128)(2,1)S(1)} %bitcast.2) | data formatting | bytes 33554432
  (2 shorter events, 0.0 us)
Async XLA Ops:
  428.2 15.7 %copy-start = (f32[2,512,1024]{2,1,0:T(8,128)S(1)}, f32[2,512,1024]{2,1,0:T(8,128)}, u32[]{:S(2)}) copy-start(f32[2,512,1024]{2,1,0:T(8,128)} %refs_8_.1) | copy-start | bytes 12582916
  428.2 15.7 %copy-start.1 = (f32[2,512,1024]{2,1,0:T(8,128)S(1)}, f32[2,512,1024]{2,1,0:T(8,128)}, u32[]{:S(2)}) copy-start(f32[2,512,1024]{2,1,0:T(8,128)} %refs_11_.1) | copy-start | bytes 12582916
  428.2 15.8 %copy-start.2 = (bf16[2,512,1024]{2,1,0:T(8,128)(2,1)S(1)}, bf16[2,512,1024]{2,1,0:T(8,128)(2,1)}, u32[]{:S(2)}) copy-start(bf16[2,512,1024]{2,1,0:T(8,128)(2,1)} %get-tuple-element.22) | copy-start | bytes 6291460
  443.9 22.6 %slice-start.4 = ((s8[16777216]{0:T(1024)(128)(4,1)}), s8[4194304]{0:T(1024)(128)(4,1)S(1)}, s32[]{:S(2)}) async-start(s8[16777216]{0:T(1024)(128)(4,1)} %bitcast.3), calls=%async_computation.4 | async-start | bytes 8388608
  443.9 22.6 %slice-start.5 = ((s8[16777216]{0:T(1024)(128)(4,1)}), s8[4194304]{0:T(1024)(128)(4,1)S(1)}, s32[]{:S(2)}) async-start(s8[16777216]{0:T(1024)(128)(4,1)} %bitcast.3), calls=%async_computation.5 | async-start | bytes 8388608
  449.6 17.0 %slice-start.6 = ((s8[16777216]{0:T(1024)(128)(4,1)}), s8[4194304]{0:T(1024)(128)(4,1)S(1)}, s32[]{:S(2)}) async-start(s8[16777216]{0:T(1024)(128)(4,1)} %bitcast.3), calls=%async_computation.6 | async-start | bytes 8388608
  449.6 17.0 %slice-start.7 = ((s8[16777216]{0:T(1024)(128)(4,1)}), s8[4194304]{0:T(1024)(128)(4,1)S(1)}, s32[]{:S(2)}) async-start(s8[16777216]{0:T(1024)(128)(4,1)} %bitcast.3), calls=%async_computation.7 | async-start | bytes 8388608
  449.6 25.5 %slice-start = ((s8[16777216]{0:T(1024)(128)(4,1)}), s8[4194304]{0:T(1024)(128)(4,1)S(1)}, s32[]{:S(2)}) async-start(s8[16777216]{0:T(1024)(128)(4,1)} %bitcast.1), calls=%async_computation | async-start | bytes 8388608
  449.6 25.5 %slice-start.1 = ((s8[16777216]{0:T(1024)(128)(4,1)}), s8[4194304]{0:T(1024)(128)(4,1)S(1)}, s32[]{:S(2)}) async-start(s8[16777216]{0:T(1024)(128)(4,1)} %bitcast.1), calls=%async_computation.1 | async-start | bytes 8388608
  466.6 8.5 %slice-start.2 = ((s8[16777216]{0:T(1024)(128)(4,1)}), s8[4194304]{0:T(1024)(128)(4,1)S(1)}, s32[]{:S(2)}) async-start(s8[16777216]{0:T(1024)(128)(4,1)} %bitcast.1), calls=%async_computation.2 | async-start | bytes 8388608
  466.6 9.5 %slice-start.3 = ((s8[16777216]{0:T(1024)(128)(4,1)}), s8[4194304]{0:T(1024)(128)(4,1)S(1)}, s32[]{:S(2)}) async-start(s8[16777216]{0:T(1024)(128)(4,1)} %bitcast.1), calls=%async_computation.3 | async-start | bytes 8388608

commit v2 on v1

--- a/solution.py
+++ b/solution.py
@@ -7,9 +7,11 @@
 from jax.experimental.pallas import tpu as pltpu
 from jax.sharding import PartitionSpec as P
 
+
 BF, F32 = jnp.bfloat16, jnp.float32
 RING = 4
 FEED = 2
+KEPT = 2
 ME, XN, YN, DG = range(4)
 XD, XO, XT, YD, YO, YT = range(6)
 
@@ -22,7 +24,7 @@
     it = iter(refs)
     take = lambda k: [next(it) for _ in range(k)]
     g, w, m, v = take(3), take(3), take(3), take(3)
-    whole, gsum, factor_ref = take(3), take(3), next(it)
+    whole, ends, gsum, factor_ref = take(KEPT), take(2), take(3), next(it)
     pair, land = take(3), take(3)
     gring, mring, vring, wring = take(2), take(2), take(2), take(2)
     squares, factor_v = take(2)
@@ -202,12 +204,14 @@
     def own_copies(u, h):
         i, layer = units[u]
         src = pair[i].at[DG, layer, h]
+        if i >= KEPT:
+            return [functools.partial(pltpu.make_async_copy, src, ends[h].at[layer], loc_s.at[1, u, h])]
         dst = out(i, layer, me, h)
         return [
+            functools.partial(pltpu.make_async_copy, src, dst, loc_s.at[1, u, h]),
             functools.partial(remote, src, dst, own_s.at[0, u, h], own_r.at[0, u, h], xnbr),
             functools.partial(remote, src, dst, own_s.at[1, u, h], own_r.at[1, u, h], ynbr),
             functools.partial(remote, src, dst, rel_s.at[ME, u, h], rel_r.at[ME, u, h], mate),
-            functools.partial(pltpu.make_async_copy, src, dst, loc_s.at[1, u, h]),
         ]
 
     for k, (u, h) in enumerate(fed):
@@ -256,7 +260,8 @@
         there = out(i, layer, owners[(XN, YN)[which]](core), h)
         remote(there, there, own_s.at[which, u, h], own_r.at[which, u, h], (xnbr, ynbr)[which]).wait_recv()
 
-    for u in range(len(units)):
+    gathered = [u for u in range(len(units)) if units[u][0] < KEPT]
+    for u in gathered:
         from_link(u, 0, 0)
         onward(u, 0, XN, 1, ynbr)
         relay(u, 0, XN)
@@ -267,7 +272,7 @@
         relay(u, 1, YN)
         from_link(u, 1, 0)
         relay(u, 1, XN)
-    for u in range(len(units)):
+    for u in gathered:
         i, layer = units[u]
         for h, to, device in ((0, 1, ynbr), (1, 0, xnbr)):
             there = out(i, layer, owners[DG](core), h)
@@ -278,11 +283,11 @@
         copy.wait_send()
     for u, h in fed:
         i, layer = units[u]
-        for copy in own_copies(u, h)[:3]:
+        own_copies(u, h)[0]().wait()
+        for copy in own_copies(u, h)[1:]:
             copy().wait_send()
-        own_copies(u, h)[3]().wait()
         pltpu.make_async_copy(pair[i].at[ME, layer, h], gsum[i].at[layer, pl.ds(h * half[i], half[i])], loc_s.at[0, u, h]).wait()
-        for block in range(4):
+        for block in range(4) if i < KEPT else ():
             there = out(i, layer, owners[block](1 - core), h)
             remote(there, there, rel_s.at[block, u, h], rel_r.at[block, u, h], mate).wait_recv()
     for k in range(1, n):
@@ -290,6 +295,97 @@
     done = pltpu.make_async_copy(factor_v, factor_ref, loc_s.at[0, 0, 0])
     done.start()
     done.wait()
+
+
+def move_kernel(*refs, parts):
+    k = (len(refs) - 3) // 2
+    src, dst, (buf, in_s, out_s) = refs[:k], refs[k : 2 * k], refs[2 * k :]
+    pieces = []
+    for a in range(k):
+        layers, height = src[a].shape[:2]
+        size = height // parts
+        pieces += [(a, layer, pl.ds(p * size, size)) for layer in range(layers) for p in range(parts)]
+    load = lambda z: pltpu.make_async_copy(src[pieces[z][0]].at[pieces[z][1], pieces[z][2]], buf.at[z], in_s.at[z])
+    store = lambda z: pltpu.make_async_copy(buf.at[z], dst[pieces[z][0]].at[pieces[z][1], pieces[z][2]], out_s.at[z])
+    for z in range(len(pieces)):
+        load(z).start()
+    for z in range(len(pieces)):
+        load(z).wait()
+        store(z).start()
+    for z in range(len(pieces)):
+        store(z).wait()
+
+
+def move(*arrays, parts=4):
+    layers, height, width = arrays[0].shape
+    pieces = len(arrays) * layers * parts
+    size = sum(a.size * 4 for a in arrays)
+    return pl.pallas_call(
+        functools.partial(move_kernel, parts=parts),
+        name="move",
+        out_shape=[jax.ShapeDtypeStruct(a.shape, a.dtype) for a in arrays],
+        in_specs=[pl.BlockSpec(memory_space=pl.ANY)] * len(arrays),
+        out_specs=[pl.BlockSpec(memory_space=pl.ANY)] * len(arrays),
+        scratch_shapes=[
+            pltpu.VMEM((pieces, height // parts, width), arrays[0].dtype),
+            pltpu.SemaphoreType.DMA((pieces,)),
+            pltpu.SemaphoreType.DMA((pieces,)),
+        ],
+        compiler_params=pltpu.CompilerParams(vmem_limit_bytes=48 * 2**20),
+        cost_estimate=cost(size),
+    )(*arrays)
+
+
+def cost(size):
+    return pl.CostEstimate(flops=size * 12, bytes_accessed=size, transcendentals=0)
+
+
+def place_kernel(*refs, spots, grown):
+    k = len(spots)
+    src, dst, (buf, in_s, out_s) = refs[:k], refs[k + grown], refs[k + grown + 1 :]
+    me = lax.axis_index("dp")
+    core, chip = me % 2, me // 2
+    cy, cx = chip % 2, chip // 2
+    layers, height = src[0].shape[:2]
+
+    def store(z, layer):
+        block, other, h = spots[z]
+        x = 1 - cx if block in (XN, DG) else cx
+        y = 1 - cy if block in (YN, DG) else cy
+        owner = 4 * x + 2 * y + (1 - core if other else core)
+        rows = pl.ds(pl.multiple_of((2 * owner + h) * height, height), height)
+        return pltpu.make_async_copy(buf.at[z, layer], dst.at[layer, rows], out_s.at[z, layer])
+
+    load = lambda z, layer: pltpu.make_async_copy(src[z].at[layer], buf.at[z, layer], in_s.at[z, layer])
+    every = [(z, layer) for z in range(k) for layer in range(layers)]
+    for one in every:
+        load(*one).start()
+    for one in every:
+        load(*one).wait()
+        store(*one).start()
+    for one in every:
+        store(*one).wait()
+
+
+def place(pieces, shape, into=None):
+    spots, arrays = zip(*pieces)
+    grown = into is not None
+    size = sum(a.size * 4 for a in arrays)
+    return pl.pallas_call(
+        functools.partial(place_kernel, spots=spots, grown=int(grown)),
+        name="place",
+        out_shape=jax.ShapeDtypeStruct(shape, arrays[0].dtype),
+        in_specs=[pl.BlockSpec(memory_space=pl.ANY)] * (len(arrays) + grown),
+        out_specs=pl.BlockSpec(memory_space=pl.ANY),
+        scratch_shapes=[
+            pltpu.VMEM((len(arrays), *arrays[0].shape), arrays[0].dtype),
+            pltpu.SemaphoreType.DMA((len(arrays), shape[0])),
+            pltpu.SemaphoreType.DMA((len(arrays), shape[0])),
+        ],
+        input_output_aliases={len(arrays): 0} if grown else {},
+        compiler_params=pltpu.CompilerParams(vmem_limit_bytes=32 * 2**20),
+        cost_estimate=cost(size),
+    )(*arrays, *((into,) if grown else ()))
 
 
 def solution(mesh):
@@ -307,11 +403,12 @@
         out = pl.pallas_call(
             functools.partial(kernel, n=n, layers=layers, count=count),
             name="step",
-            out_shape=[jax.ShapeDtypeStruct(one.shape, BF) for one in weights]
+            out_shape=[jax.ShapeDtypeStruct(one.shape, BF) for one in weights[:KEPT]]
+            + [jax.ShapeDtypeStruct((layers, *blocks[KEPT]), BF)] * 2
             + [jax.ShapeDtypeStruct(one.shape, BF) for one in m]
             + [jax.ShapeDtypeStruct((8, 128), F32)],
             in_specs=[any_space] * 12,
-            out_specs=[any_space] * 7,
+            out_specs=[any_space] * (KEPT + 6),
             scratch_shapes=[pltpu.VMEM((4, layers, 2, *b), BF) for b in blocks]
             + [pltpu.VMEM((6, layers, *b), BF) for b in blocks]
             + [pltpu.VMEM((RING, *b), BF) for b in kinds]
@@ -323,9 +420,37 @@
             + [dma((4, units, 2)), dma((4, units, 2)), dma((2, units, 2))],
             compiler_params=pltpu.CompilerParams(collective_id=0, has_side_effects=True, vmem_limit_bytes=62 * 2**20),
         )(*terms, *weights, *m, *v)
-        whole, sums, factor = out[:3], out[3:6], out[6][0, 0]
-        new = [moments(a, b, s.astype(F32) * factor) for a, b, s in zip(m, v, sums, strict=True)]
-        return (*whole, *(one[0] for one in new), *(one[1] for one in new))
+        kept, (low, high), sums, factor = out[:KEPT], out[KEPT : KEPT + 2], out[KEPT + 2 : KEPT + 5], out[KEPT + 5][0, 0]
+
+        def hop(a, flip):
+            return lax.ppermute(a, "dp", [(i, i ^ flip) for i in range(n)])
+
+        def fresh(i):
+            return moments(m[i], v[i], sums[i].astype(F32) * factor)
+
+        x, y, mate = n // 2, n // 4, 1
+        x_low, y_high = hop(low, x), hop(high, y)
+        m_low, m_high = hop(low, mate), hop(high, mate)
+        x_high, y_low = hop(high, x), hop(low, y)
+        new = [fresh(0), fresh(1)]
+        x_low, y_high, new = lax.optimization_barrier((x_low, y_high, new))
+        d_low, d_high = hop(x_low, y), hop(y_high, x)
+        mx_low, my_high = hop(x_low, mate), hop(y_high, mate)
+        kept = move(*kept)
+        new.append(fresh(2))
+        x_high, y_low, kept, new = lax.optimization_barrier((x_high, y_low, kept, new))
+        mx_high, my_low = hop(x_high, mate), hop(y_low, mate)
+        shape = weights[KEPT].shape
+        first = [((ME, 0, 0), low), ((ME, 0, 1), high), ((ME, 1, 0), m_low), ((ME, 1, 1), m_high), ((XN, 0, 0), x_low), ((YN, 0, 1), y_high)]
+        first += [((XN, 1, 0), mx_low), ((YN, 1, 1), my_high)]
+        down = place(first, shape)
+        then = [((XN, 0, 1), x_high), ((YN, 0, 0), y_low), ((XN, 1, 1), mx_high), ((YN, 1, 0), my_low)]
+        down = place(then, shape, down)
+        d_low, d_high, down = lax.optimization_barrier((d_low, d_high, down))
+        md_low, md_high = hop(d_low, mate), hop(d_high, mate)
+        last = [((DG, 0, 0), d_low), ((DG, 0, 1), d_high), ((DG, 1, 0), md_low), ((DG, 1, 1), md_high)]
+        down = place(last, shape, down)
+        return (*kept, down, *(one[0] for one in new), *(one[1] for one in new))
 
     all_of, cut = P(None, None, None), P(None, "dp", None)
     return jax.shard_map(

time: 483 us -> 474 us (0.981)
  waiting for transfers between devices: 0 us -> 48.5 us
  Pallas kernels: 426 us -> 391 us
  local copies, waits for them, and re-layouts: 33.8 us -> 1.2 us
  starting transfers between devices: 0 us -> 7.98 us
    pallas_call x1, Pallas kernels: 426 us -> 359 us  [step(): pl.pallas_call(functools.partial(kernel, n=n, layers=layers, count=count)...]
    ppermute x0 -> x14, waiting for transfers between devices: none -> 48.5 us  [hop(): return lax.ppermute(a, 'dp', [(i, i ^ flip) for i in range(n)])]
    unnamed x25 -> x8, local copies, waits for them, and re-layouts: 32.6 us -> 0.01 us
    pallas_call x0 -> x4, Pallas kernels: none -> 31.7 us  [the longest x1 22.7 us: move(): pl.pallas_call(functools.partial(move_kernel, parts=parts), name='move',...]
    ppermute x0 -> x14, starting transfers between devices: none -> 7.98 us  [hop(): return lax.ppermute(a, 'dp', [(i, i ^ flip) for i in range(n)])]
  transfers between devices with their start and end apart: 0 -> 14, of which waited for: 0 -> 6; matrix products, arithmetic and copies ran while one was open for 0% -> 5% of each run, Pallas kernels for 0% -> 6%
where the time goes in v2:
time: 474 us
  Pallas kernels  391 us (82%)
  waiting for transfers between devices  48.5 us (10%)
  other arithmetic  24.1 us (5%)
  starting transfers between devices  7.98 us (2%)
    pallas_call x1, Pallas kernels, step(): pl.pallas_call(functools.partial(kernel, n=n, layers=layers, count=count)...  359 us
    ppermute x14, waiting for transfers between devices, hop(): return lax.ppermute(a, 'dp', [(i, i ^ flip) for i in range(n)])  48.5 us
    add x2, other arithmetic, moments(): return (0.9 * m + 0.1 * g, 0.95 * v + 0.05 * g * g)  24.1 us
    pallas_call x1, Pallas kernels, move(): pl.pallas_call(functools.partial(move_kernel, parts=parts), name='move',...  22.7 us
  transfers between devices with their start and end apart: 14, of which 6 were waited for; matrix products, arithmetic and copies ran while one was open for 5% of the time, Pallas kernels for 6%

profile of v2, /device:TPU:0, one launch (start us, length us, event | category | flops | bytes accessed | tf_op | source)
XLA Modules:
  0.0 473.8 jit_solution(11435509875796911273)
XLA Ops:
  0.6 359.5 %step.1 = (bf16[2,1024,4096]{2,1,0:T(8,128)(2,1)}, bf16[2,1024,4096]{2,1,0:T(8,128)(2,1)}, bf16[2,256,1024]{2,1,0:T(8,128)(2,1)}, bf16[2,256,1024]{2,1,0:T(8,128...) custom-call(bf16[1,2,1024,4096]{3,2,1,0:T(8,128)(2,1)} %refs_0_.1, ...), custom_call_target="tpu_custom_call" | custom-call | tf_op jit(solution)/shard_map/step/pallas_call | solution.py:403
  360.1 0.3 collective-permute-start.9
  360.4 1.4 collective-permute-start.3
  361.8 1.4 collective-permute-start
  363.2 0.6 collective-permute-start.2
  363.8 0.7 collective-permute-start.1
  364.5 1.2 slice.3
  365.7 0.0 copy-start
  365.7 0.0 copy-start.2
  365.7 0.0 copy-start.3
  365.7 15.7 %fusion = (f32[2,128,4096]{2,1,0:T(8,128)}, f32[2,128,4096]{2,1,0:T(8,128)}, f32[2,128,4096]{2,1,0:T(8,128)}, f32[2,128,4096]{2,1,0:T(8,128)}) fusion(f32[2,128,4096]{2,1,0:T(8,128)} %refs_9_.1, bf16[2,128,4096]{2,1,0:T(8,128)(2,1)} %get-tuple-element.44, f32[]{:T(128)} %bitcast, f32[2,128,4096]{2,1,0:T(8,128)} %refs_6_.1, ...), kind=kLoop, calls=%fused_computation.3 | loop fusion | flops 18874368 | bytes 37748740 | tf_op jit(solution)/shard_map/add | solution.py:20
  381.4 5.3 %collective-permute-done.3.refs_5_ = bf16[2,256,1024]{2,1,0:T(8,128)(2,1)S(1)} collective-permute-done((bf16[2,256,1024]{2,1,0:T(8,128)(2,1)}, bf16[2,256,1024]{2,1,0:T(8,128)(2,1)S(1)}, u32[]{:S(2)}, u32[]{:S(2)}) %collective-permute-start.3) | collective-permute-done | bytes 1048608 | tf_op jit(solution)/shard_map/ppermute | solution.py:426
  386.7 0.0 copy-done
  386.7 0.0 collective-permute-start.8
  386.7 22.8 %collective-permute-done.2.refs_4_ = bf16[2,256,1024]{2,1,0:T(8,128)(2,1)S(1)} collective-permute-done((bf16[2,256,1024]{2,1,0:T(8,128)(2,1)}, bf16[2,256,1024]{2,1,0:T(8,128)(2,1)S(1)}, u32[]{:S(2)}, u32[]{:S(2)}) %collective-permute-start.2) | collective-permute-done | bytes 1048608 | tf_op jit(solution)/shard_map/ppermute | solution.py:426
  409.5 0.0 collective-permute-start.10
  409.5 0.0 copy-done.2
  409.5 0.0 copy-done.3
  409.5 8.4 %fusion.2 = (f32[2,512,1024]{2,1,0:T(8,128)}, f32[2,512,1024]{2,1,0:T(8,128)}) fusion(f32[2,512,1024]{2,1,0:T(8,128)} %refs_11_.1, bf16[2,512,1024]{2,1,0:T(8,128)(2,1)S(1)} %copy-done.3, f32[]{:T(128)} %bitcast, f32[2,512,1024]{2,1,0:T(8,128)S(1)} %copy-done.2), kind=kLoop, calls=%fused_computation.5 | loop fusion | flops 9437184 | bytes 18874372 | tf_op jit(solution)/shard_map/add | solution.py:20
  417.9 0.0 collective-permute-done.refs_0_
  417.9 0.5 collective-permute-start.11
  418.4 0.0 copy-start.1
  418.4 22.7 %move.1 = (bf16[2,1024,4096]{2,1,0:T(8,128)(2,1)}, bf16[2,1024,4096]{2,1,0:T(8,128)(2,1)}) custom-call(bf16[2,1024,4096]{2,1,0:T(8,128)(2,1)} %get-tuple-element.40.refs_0_, bf16[2,1024,4096]{2,1,0:T(8,128)(2,1)} %get-tuple-element.41.refs_1_), custom_call_target="tpu_custom_call" | custom-call | flops 805306368 | bytes 67108864 | tf_op jit(solution)/shard_map/move/pallas_call | solution.py:323
  441.1 0.0 collective-permute-done.1.refs_1_
  441.2 0.0 collective-permute-start.6
  441.2 0.0 collective-permute-done.9.refs_3_
  441.2 0.5 collective-permute-start.7
  441.7 0.0 collective-permute-done.8.refs_2_
  441.7 0.7 collective-permute-start.4
  442.3 0.0 collective-permute-done.10.refs_6_
  442.3 1.5 collective-permute-start.5
  443.8 0.0 collective-permute-done.11.refs_7_
  443.8 0.0 copy-done.1
  443.8 4.1 place.3.refs_4_
  447.9 0.0 collective-permute-done.6.refs_2_
  448.0 0.0 collective-permute-done.7.refs_3_
  448.0 2.5 place.4.refs_4_
  450.4 16.4 %collective-permute-done.4.refs_0_ = bf16[2,256,1024]{2,1,0:T(8,128)(2,1)S(1)} collective-permute-done((bf16[2,256,1024]{2,1,0:T(8,128)(2,1)S(1)}, bf16[2,256,1024]{2,1,0:T(8,128)(2,1)S(1)}, u32[]{:S(2)}, u32[]{:S(2)}) %collective-permute-start.4) | collective-permute-done | bytes 1048608 | tf_op jit(solution)/shard_map/ppermute | solution.py:426
  466.8 0.4 collective-permute-done.5.refs_1_
  467.2 0.0 collective-permute-start.12
  467.2 0.5 collective-permute-start.13
  467.7 2.1 collective-permute-done.12.refs_2_
  469.8 1.5 collective-permute-done.13.refs_3_
  471.3 2.4 place.5
Async XLA Ops:
  360.1 81.1 %collective-permute-start.9 = (bf16[2,256,1024]{2,1,0:T(8,128)(2,1)}, bf16[2,256,1024]{2,1,0:T(8,128)(2,1)S(1)}, u32[]{:S(2)}, u32[]{:S(2)}) collective-permute-start(bf16[2,256,1024]{2,1,0:T(8,128)(2,1)} %get-tuple-element.38.refs_1_), channel_id=1, source_target_pairs={{0,1},{1,0},{2,3},{3,2},{4,5},{5,4},{6,7},{7,6}} | collective-permute-start | bytes 3145736 | tf_op jit(solution)/shard_map/ppermute | solution.py:426
  360.4 26.2 %collective-permute-start.3 = (bf16[2,256,1024]{2,1,0:T(8,128)(2,1)}, bf16[2,256,1024]{2,1,0:T(8,128)(2,1)S(1)}, u32[]{:S(2)}, u32[]{:S(2)}) collective-permute-start(bf16[2,256,1024]{2,1,0:T(8,128)(2,1)} %get-tuple-element.38.refs_1_), channel_id=1, source_target_pairs={{0,2},{1,3},{2,0},{3,1},{4,6},{5,7},{6,4},{7,5}} | collective-permute-start | bytes 3145736 | tf_op jit(solution)/shard_map/ppermute | solution.py:426
  361.8 56.1 %collective-permute-start = (bf16[2,256,1024]{2,1,0:T(8,128)(2,1)}, bf16[2,256,1024]{2,1,0:T(8,128)(2,1)S(1)}, u32[]{:S(2)}, u32[]{:S(2)}) collective-permute-start(bf16[2,256,1024]{2,1,0:T(8,128)(2,1)} %get-tuple-element.38.refs_1_), channel_id=1, source_target_pairs={{0,4},{1,5},{2,6},{3,7},{4,0},{5,1},{6,2},{7,3}} | collective-permute-start | bytes 3145736 | tf_op jit(solution)/shard_map/ppermute | solution.py:426
  363.2 46.3 %collective-permute-start.2 = (bf16[2,256,1024]{2,1,0:T(8,128)(2,1)}, bf16[2,256,1024]{2,1,0:T(8,128)(2,1)S(1)}, u32[]{:S(2)}, u32[]{:S(2)}) collective-permute-start(bf16[2,256,1024]{2,1,0:T(8,128)(2,1)} %get-tuple-element.39.refs_0_), channel_id=1, source_target_pairs={{0,4},{1,5},{2,6},{3,7},{4,0},{5,1},{6,2},{7,3}} | collective-permute-start | bytes 3145736 | tf_op jit(solution)/shard_map/ppermute | solution.py:426
  363.8 77.3 %collective-permute-start.1 = (bf16[2,256,1024]{2,1,0:T(8,128)(2,1)}, bf16[2,256,1024]{2,1,0:T(8,128)(2,1)S(1)}, u32[]{:S(2)}, u32[]{:S(2)}) collective-permute-start(bf16[2,256,1024]{2,1,0:T(8,128)(2,1)} %get-tuple-element.39.refs_0_), channel_id=1, source_target_pairs={{0,2},{1,3},{2,0},{3,1},{4,6},{5,7},{6,4},{7,5}} | collective-permute-start | bytes 3145736 | tf_op jit(solution)/shard_map/ppermute | solution.py:426
  365.7 21.0 %copy-start = (bf16[2,256,1024]{2,1,0:T(8,128)(2,1)S(1)}, bf16[2,256,1024]{2,1,0:T(8,128)(2,1)}, u32[]{:S(2)}) copy-start(bf16[2,256,1024]{2,1,0:T(8,128)(2,1)} %get-tuple-element.39.refs_0_) | copy-start | bytes 3145732
  365.7 43.9 %copy-start.2 = (f32[2,512,1024]{2,1,0:T(8,128)S(1)}, f32[2,512,1024]{2,1,0:T(8,128)}, u32[]{:S(2)}) copy-start(f32[2,512,1024]{2,1,0:T(8,128)} %refs_8_.1) | copy-start | bytes 12582916
  365.7 43.9 %copy-start.3 = (bf16[2,512,1024]{2,1,0:T(8,128)(2,1)S(1)}, bf16[2,512,1024]{2,1,0:T(8,128)(2,1)}, u32[]{:S(2)}) copy-start(bf16[2,512,1024]{2,1,0:T(8,128)(2,1)} %get-tuple-element.51) | copy-start | bytes 6291460
  386.7 55.0 %collective-permute-start.8 = (bf16[2,256,1024]{2,1,0:T(8,128)(2,1)S(1)}, bf16[2,256,1024]{2,1,0:T(8,128)(2,1)S(1)}, u32[]{:S(2)}, u32[]{:S(2)}) collective-permute-start(bf16[2,256,1024]{2,1,0:T(8,128)(2,1)S(1)} %copy-done), channel_id=1, source_target_pairs={{0,1},{1,0},{2,3},{3,2},{4,5},{5,4},{6,7},{7,6}} | collective-permute-start | bytes 3145736 | tf_op jit(solution)/shard_map/ppermute | solution.py:426
  409.5 32.8 %collective-permute-start.10 = (bf16[2,256,1024]{2,1,0:T(8,128)(2,1)S(1)}, bf16[2,256,1024]{2,1,0:T(8,128)(2,1)S(1)}, u32[]{:S(2)}, u32[]{:S(2)}) collective-permute-start(bf16[2,256,1024]{2,1,0:T(8,128)(2,1)S(1)} %collective-permute-done.2.refs_4_), channel_id=1, source_target_pairs={{0,1},{1,0},{2,3},{3,2},{4,5},{5,4},{6,7},{7,6}} | collective-permute-start | bytes 3145736 | tf_op jit(solution)/shard_map/ppermute | solution.py:426
  417.9 25.9 %collective-permute-start.11 = (bf16[2,256,1024]{2,1,0:T(8,128)(2,1)S(1)}, bf16[2,256,1024]{2,1,0:T(8,128)(2,1)S(1)}, u32[]{:S(2)}, u32[]{:S(2)}) collective-permute-start(bf16[2,256,1024]{2,1,0:T(8,128)(2,1)S(1)} %collective-permute-done.3.refs_5_), channel_id=1, source_target_pairs={{0,1},{1,0},{2,3},{3,2},{4,5},{5,4},{6,7},{7,6}} | collective-permute-start | bytes 3145736 | tf_op jit(solution)/shard_map/ppermute | solution.py:426
  418.4 25.4 %copy-start.1 = (bf16[2,256,1024]{2,1,0:T(8,128)(2,1)S(1)}, bf16[2,256,1024]{2,1,0:T(8,128)(2,1)}, u32[]{:S(2)}) copy-start(bf16[2,256,1024]{2,1,0:T(8,128)(2,1)} %get-tuple-element.38.refs_1_) | copy-start | bytes 3145732
  441.2 6.8 %collective-permute-start.6 = (bf16[2,256,1024]{2,1,0:T(8,128)(2,1)S(1)}, bf16[2,256,1024]{2,1,0:T(8,128)(2,1)S(1)}, u32[]{:S(2)}, u32[]{:S(2)}) collective-permute-start(bf16[2,256,1024]{2,1,0:T(8,128)(2,1)S(1)} %collective-permute-done.refs_0_), channel_id=1, source_target_pairs={{0,1},{1,0},{2,3},{3,2},{4,5},{5,4},{6,7},{7,6}} | collective-permute-start | bytes 3145736 | tf_op jit(solution)/shard_map/ppermute | solution.py:426
  441.2 6.8 %collective-permute-start.7 = (bf16[2,256,1024]{2,1,0:T(8,128)(2,1)S(1)}, bf16[2,256,1024]{2,1,0:T(8,128)(2,1)S(1)}, u32[]{:S(2)}, u32[]{:S(2)}) collective-permute-start(bf16[2,256,1024]{2,1,0:T(8,128)(2,1)S(1)} %collective-permute-done.1.refs_1_), channel_id=1, source_target_pairs={{0,1},{1,0},{2,3},{3,2},{4,5},{5,4},{6,7},{7,6}} | collective-permute-start | bytes 3145736 | tf_op jit(solution)/shard_map/ppermute | solution.py:426
  441.7 25.1 %collective-permute-start.4 = (bf16[2,256,1024]{2,1,0:T(8,128)(2,1)S(1)}, bf16[2,256,1024]{2,1,0:T(8,128)(2,1)S(1)}, u32[]{:S(2)}, u32[]{:S(2)}) collective-permute-start(bf16[2,256,1024]{2,1,0:T(8,128)(2,1)S(1)} %collective-permute-done.2.refs_4_), channel_id=1, source_target_pairs={{0,2},{1,3},{2,0},{3,1},{4,6},{5,7},{6,4},{7,5}} | collective-permute-start | bytes 3145736 | tf_op jit(solution)/shard_map/ppermute | solution.py:426
  442.3 24.8 %collective-permute-start.5 = (bf16[2,256,1024]{2,1,0:T(8,128)(2,1)S(1)}, bf16[2,256,1024]{2,1,0:T(8,128)(2,1)S(1)}, u32[]{:S(2)}, u32[]{:S(2)}) collective-permute-start(bf16[2,256,1024]{2,1,0:T(8,128)(2,1)S(1)} %collective-permute-done.3.refs_5_), channel_id=1, source_target_pairs={{0,4},{1,5},{2,6},{3,7},{4,0},{5,1},{6,2},{7,3}} | collective-permute-start | bytes 3145736 | tf_op jit(solution)/shard_map/ppermute | solution.py:426
  467.2 2.7 collective-permute-start.12
  467.2 4.2 collective-permute-start.13

commit v3 on v0

v3 whole, which is shorter than its diff:
```python
import functools
from typing import NamedTuple

import jax
import jax.numpy as jnp
from jax import lax
from jax.experimental import pallas as pl
from jax.experimental.pallas import tpu as pltpu
from jax.sharding import PartitionSpec as P


BF, F32 = jnp.bfloat16, jnp.float32
RING = 4
FEED = (3, 2)
KEPT = 2
CUT = 4
ME, XN, YN, DG = range(4)
XD, XO, XT, YD, YO, YT = range(6)


def moments(m, v, g):
    return 0.9 * m + 0.1 * g, 0.95 * v + 0.05 * g * g


def neighbours():
    me = lax.axis_index("dp")
    core, chip = me % 2, me // 2
    cy, cx = chip % 2, chip // 2
    owner = lambda block, c: 4 * (1 - cx if block in (XN, DG) else cx) + 2 * (1 - cy if block in (YN, DG) else cy) + c
    return me, core, owner


def kernel(*refs, n, layers, count):
    it = iter(refs)
    take = lambda k: [next(it) for _ in range(k)]
    g, w, m, v = take(3), take(3), take(3), take(3)
    whole, ends, mates, parts, tails, gsum, factor_ref = take(KEPT), take(2), take(2), take(2), take(2), take(3), next(it)
    pair, land = take(3), take(3)
    gring, mring, vring, wring = take(2), take(2), take(2), take(2)
    squares, factor_v = take(2)
    d2d_s, d2d_r, lk_s, lk_r, ring_s, feed_s = take(6)
    sq_s, own_s, fwd_s, rel_s, loc_s, end_s, end_r = take(7)

    me, core, owner = neighbours()
    mate, xnbr, ynbr = owner(ME, 1 - core), owner(XN, core), owner(YN, core)
    across = (xnbr, ynbr)

    def remote(src, dst, s, r, device):
        return pltpu.make_async_remote_copy(
            src_ref=src, dst_ref=dst, send_sem=s, recv_sem=r, device_id={"dp": device}, device_id_type=pl.DeviceIdType.MESH
        )

    barrier = pltpu.get_barrier_semaphore()
    for k in range(1, n):
        pl.semaphore_signal(barrier, inc=1, device_id={"dp": (me + k) % n}, device_id_type=pl.DeviceIdType.MESH)

    units, kind, half = geometry(land, layers)

    def rows(i, device, r0=0, nr=None):
        return pl.ds(pl.multiple_of(device * (2 * half[i]) + r0, 16), 2 * half[i] if nr is None else nr)

    steps = rs_steps(units, half)
    exchanges = exchange_list(steps, half, units)

    def part(step):
        return pair[units[step.u][0]].at[step.block, units[step.u][1], pl.ds(step.h * half[units[step.u][0]] + step.r0, step.nr)]

    def exchange(z):
        block, u, r0, nr = exchanges[z]
        i, layer = units[u]
        src = g[i].at[0, layer, rows(i, owner(block, 1 - core), r0, nr)]
        return remote(src, pair[i].at[block, layer, pl.ds(r0, nr)], d2d_s.at[i], d2d_r.at[z], mate)

    order = {c: [k for k, step in enumerate(steps) if kind[units[step.u][0]] == c] for c in (0, 1)}
    place_of = {k: (c, p) for c in order for p, k in enumerate(order[c])}

    def own_rows(k):
        c, p = place_of[k]
        return gring[c].at[p % RING, pl.ds(0, steps[k].nr)]

    def term(k):
        step = steps[k]
        i, layer = units[step.u]
        c, p = place_of[k]
        src = g[i].at[0, layer, rows(i, owner(step.block, core), step.h * half[i] + step.r0, step.nr)]
        return pltpu.make_async_copy(src, own_rows(k), ring_s.at[c, p % RING])

    def landed(step, stream):
        i, layer = units[step.u]
        return land[i].at[stream, layer, pl.ds(step.r0, step.nr)]

    def push(k):
        step = steps[k]
        return remote(part(step), landed(step, step.stream), lk_s.at[units[step.u][0]], lk_r.at[k], across[step.stream >= YD])

    seen, met = set(), set()

    def arrive(stream, step):
        for k, other in enumerate(steps):
            overlap = other.r0 < step.r0 + step.nr and step.r0 < other.r0 + other.nr
            if other.send and other.stream == stream and other.u == step.u and overlap and k not in seen:
                seen.add(k)
                dst = landed(other, stream)
                remote(dst, dst, lk_s.at[0], lk_r.at[k], xnbr).wait_recv()

    def meet(step):
        first = step.h * half[units[step.u][0]] + step.r0
        for z, (block, u, r0, nr) in enumerate(exchanges):
            if block == step.block and u == step.u and r0 < first + step.nr and first < r0 + nr and z not in met:
                met.add(z)
                i, layer = units[u]
                dst = pair[i].at[block, layer, pl.ds(r0, nr)]
                remote(dst, dst, d2d_s.at[0], d2d_r.at[z], mate).wait_recv()

    fed = make_order(units, half)
    feed_order = {c: [k for k, piece in enumerate(fed) if kind[units[piece[0]][0]] == c] for c in (0, 1)}
    feed_at = {k: p for c in (0, 1) for p, k in enumerate(feed_order[c])}

    def feed_slot(k):
        c = kind[units[fed[k][0]][0]]
        return [ring[c].at[feed_at[k] % FEED[c], pl.ds(0, fed[k][3])] for ring in (mring, vring, wring)]

    def feed(k):
        u, h, r0, nr = fed[k]
        i, layer = units[u]
        c = kind[i]
        slot = feed_at[k] % FEED[c]
        mine = pl.ds(h * half[i] + r0, nr)
        src = (m[i].at[layer, mine], v[i].at[layer, mine], w[i].at[layer, rows(i, me, h * half[i] + r0, nr)])
        return [pltpu.make_async_copy(a, b, feed_s.at[z, c, slot]) for z, (a, b) in enumerate(zip(src, feed_slot(k), strict=True))]

    exchanged, started = 0, {0: 0, 1: 0}

    def next_exchange():
        nonlocal exchanged
        if exchanged < len(exchanges):
            exchange(exchanged).start()
            exchanged += 1

    def next_term(c):
        if started[c] < len(order[c]):
            term(order[c][started[c]]).start()
            started[c] += 1

    next_term(0)
    next_term(0)
    pl.semaphore_wait(barrier, n - 1)
    for _ in range(4):
        next_exchange()
    next_term(0)
    next_term(0)

    def tile_of(cols, nr):
        return min(65536 // cols, nr)

    zero = jnp.zeros((8, 128), F32)
    total = (zero,) * 4
    for k, step in enumerate(steps):
        i, layer = units[step.u]
        c = kind[i]
        dst = part(step)
        meet(step)
        term(k).wait()
        more = []
        for stream in step.needs:
            arrive(stream, step)
            more.append(landed(step, stream))
        own = own_rows(k)
        cols = dst.shape[1]
        tile = tile_of(cols, step.nr)

        def body(r, acc, dst=dst, own=own, more=more, cols=cols, tile=tile, squared=not step.send):
            at_rows = pl.ds(pl.multiple_of(r * tile, tile), tile)
            s = own[at_rows, :].astype(F32) + dst[at_rows, :].astype(F32)
            for one in more:
                s = s + one[at_rows, :].astype(F32)
            b = s.astype(BF)
            dst[at_rows, :] = b
            if squared:
                q = b.astype(F32)
                q = q * q
                acc = list(acc)
                for a in range(tile // 8):
                    for z in range(cols // 128):
                        acc[(a + z) % 4] = acc[(a + z) % 4] + q[8 * a : 8 * a + 8, 128 * z : 128 * z + 128]
                acc = tuple(acc)
            return acc

        if step.send:
            lax.fori_loop(0, step.nr // tile, body, ())
            push(k).start()
        else:
            total = lax.fori_loop(0, step.nr // tile, body, total)
            pltpu.make_async_copy(dst, gsum[i].at[layer, pl.ds(step.h * half[i] + step.r0, step.nr)], loc_s.at[0, i]).start()
        next_term(c)
        next_exchange()
        if k == 5:
            for _ in range(RING):
                next_term(1)
        if k == 20:
            for c in (0, 1):
                for z in feed_order[c][: FEED[c]]:
                    for copy in feed(z):
                        copy.start()

    squares[n] = total[0] + total[1] + total[2] + total[3]
    for k in range(1, n):
        remote(squares.at[n], squares.at[me], sq_s.at[0], sq_s.at[1], (me + k) % n).start()
    for i in range(3):
        remote(pair[i], pair[i], d2d_s.at[i], d2d_r.at[0], mate).wait_send()
        remote(land[i], land[i], lk_s.at[i], lk_r.at[0], xnbr).wait_send()
    squares[me] = squares[n]
    others = squares.at[pl.ds(0, n - 1)]
    remote(others, others, sq_s.at[0], sq_s.at[1], xnbr).wait_recv()
    everything = squares[0]
    for k in range(1, n):
        everything = everything + squares[k]
    everything = jnp.sum(jnp.sum(everything, axis=0, keepdims=True), axis=1, keepdims=True)
    factor = jnp.minimum(1.0, 0.5 * lax.rsqrt(everything / count + 1e-30))
    factor_v[...] = jnp.broadcast_to(factor, (8, 128))

    def out(i, layer, device, r0=0, nr=None):
        return whole[i].at[layer, rows(i, device, r0, nr)]

    gathered = [u for u in range(len(units)) if units[u][0] < KEPT]
    sent = [k for k, piece in enumerate(fed) if piece[0] in gathered]

    for k, (u, h, r0, nr) in enumerate(fed):
        i, layer = units[u]
        c = kind[i]
        for copy in feed(k):
            copy.wait()
        mine = pl.ds(h * half[i] + r0, nr)
        dst, src = pair[i].at[DG, layer, mine], pair[i].at[ME, layer, mine]
        mm, vv, ww = feed_slot(k)
        tile = min(32768 // dst.shape[1] if c else 16, nr)

        def body(r, _, dst=dst, src=src, mm=mm, vv=vv, ww=ww, tile=tile):
            at_rows = pl.ds(pl.multiple_of(r * tile, tile), tile)
            grad = src[at_rows, :].astype(F32) * factor_v[0:1, 0:1]
            m_new, v_new = moments(mm[at_rows, :], vv[at_rows, :], grad)
            weight = ww[at_rows, :].astype(F32)
            dst[at_rows, :] = (weight - 0.02 * (m_new * lax.rsqrt(v_new + 1e-8) + 0.1 * weight)).astype(BF)
            return 0

        lax.fori_loop(0, nr // tile, body, 0)
        if i < KEPT:
            here = out(i, layer, me, h * half[i] + r0, nr)
            z = sent.index(k)
            remote(dst, here, own_s.at[0, i], lk_r.at[z], xnbr).start()
            remote(dst, here, own_s.at[1, i], lk_r.at[len(sent) + z], ynbr).start()
            remote(dst, here, own_s.at[2, i], d2d_r.at[z], mate).start()
            pltpu.make_async_copy(dst, here, loc_s.at[1, i]).start()
        else:
            remote(dst, mates[h].at[layer], end_s.at[0, h], end_r.at[0, h], mate).start()
            pltpu.make_async_copy(dst, ends[h].at[layer], loc_s.at[2, h]).start()
            tail = half[i] // CUT
            pltpu.make_async_copy(dst.at[pl.ds(0, half[i] - tail)], parts[h].at[layer], loc_s.at[3, h]).start()
        if feed_at[k] + FEED[c] < len(feed_order[c]):
            for copy in feed(feed_order[c][feed_at[k] + FEED[c]]):
                copy.start()

    relays = [(u, h, block) for u in gathered for h in range(2) for block in (XN, YN, DG)]

    def relay(u, h, block):
        i, layer = units[u]
        here = out(i, layer, owner(block, core), h * half[i], half[i])
        remote(here, here, rel_s.at[block - 1, i], d2d_r.at[len(sent) + relays.index((u, h, block))], mate).start()

    def forward_sem(u, h):
        return lk_r.at[2 * len(sent) + 2 * u + h]

    def onward(u, h, block, device):
        i, layer = units[u]
        here = out(i, layer, owner(block, core), h * half[i], half[i])
        remote(here, here, fwd_s.at[h, i], forward_sem(u, h), device).start()

    def from_link(u, h, which):
        i, layer = units[u]
        for z, k in enumerate(sent):
            if fed[k][:2] == (u, h):
                there = out(i, layer, owner((XN, YN)[which], core), h * half[i] + fed[k][2], fed[k][3])
                remote(there, there, own_s.at[0, 0], lk_r.at[which * len(sent) + z], xnbr).wait_recv()

    for u in gathered:
        from_link(u, 0, 0)
        onward(u, 0, XN, ynbr)
        relay(u, 0, XN)
        from_link(u, 1, 1)
        onward(u, 1, YN, xnbr)
        relay(u, 1, YN)
        from_link(u, 0, 1)
        relay(u, 0, YN)
        from_link(u, 1, 0)
        relay(u, 1, XN)

    for u, (i, layer) in enumerate(units):
        if i >= KEPT:
            tail = half[i] // CUT
            for h in range(2):
                src = pair[i].at[DG, layer, pl.ds((h + 1) * half[i] - tail, tail)]
                remote(src, tails[h].at[layer], end_s.at[1, h], end_r.at[1, h], across[h]).start()

    for u in gathered:
        i, layer = units[u]
        for h in range(2):
            there = out(i, layer, owner(DG, core), h * half[i], half[i])
            remote(there, there, fwd_s.at[0, 0], forward_sem(u, h), xnbr).wait_recv()
            relay(u, h, DG)

    for i in range(3):
        pltpu.make_async_copy(gsum[i], gsum[i], loc_s.at[0, i]).wait()
    for i in range(KEPT):
        block, part_of = whole[i].at[:, pl.ds(0, 2 * half[i])], whole[i].at[:, pl.ds(0, half[i])]
        pltpu.make_async_copy(block, block, loc_s.at[1, i]).wait()
        for z in range(3):
            remote(block, block, own_s.at[z, i], lk_r.at[0], xnbr).wait_send()
        for h in range(2):
            remote(part_of, part_of, fwd_s.at[h, i], lk_r.at[0], xnbr).wait_send()
    for h in range(2):
        pltpu.make_async_copy(ends[h], ends[h], loc_s.at[2, h]).wait()
        pltpu.make_async_copy(parts[h], parts[h], loc_s.at[3, h]).wait()
        both = remote(mates[h], mates[h], end_s.at[0, h], end_r.at[0, h], mate)
        both.wait_send()
        both.wait_recv()
    remote(others, others, sq_s.at[0], sq_s.at[1], xnbr).wait_send()
    for z, k in enumerate(sent):
        u, h, r0, nr = fed[k]
        i, layer = units[u]
        there = out(i, layer, mate, h * half[i] + r0, nr)
        remote(there, there, own_s.at[0, 0], d2d_r.at[z], mate).wait_recv()
    done = pltpu.make_async_copy(factor_v, factor_ref, loc_s.at[0, 0])
    done.start()
    done.wait()
    for z, (u, h, block) in enumerate(relays):
        i, layer = units[u]
        there = out(i, layer, owner(block, 1 - core), h * half[i], half[i])
        remote(there, there, rel_s.at[0, 0], d2d_r.at[len(sent) + z], mate).wait_recv()
    for i in range(KEPT):
        block = whole[i].at[:, pl.ds(0, 2 * half[i])]
        for z in range(3):
            remote(block, block, rel_s.at[z, i], d2d_r.at[0], mate).wait_send()
    for h in range(2):
        both = remote(tails[h], tails[h], end_s.at[1, h], end_r.at[1, h], xnbr)
        both.wait_send()
        both.wait_recv()


class Step(NamedTuple):
    send: bool
    block: int
    u: int
    h: int
    r0: int
    nr: int
    stream: int | None
    needs: tuple


def geometry(land, layers):
    return [(i, layer) for i in range(3) for layer in range(layers)], (0, 0, 1), [p.shape[2] for p in land]


def cuts(size, shares):
    at = 0
    for share in shares:
        yield at, size * share // 4
        at += size * share // 4


def rs_steps(units, half):
    steps = []
    last = len(units) - 1

    def add(send, u, shares, *two):
        for r0, nr in cuts(half[units[u][0]], shares):
            steps.extend(Step(send, block, u, h, r0, nr, stream, needs) for block, h, stream, needs in two)

    for u in range(last + 1):
        add(True, u, (1, 1, 2) if u == 0 else (4,), (DG, 0, XD, ()), (DG, 1, YD, ()))
    for u in range(last + 1):
        add(True, u, (4,), (XN, 0, XO, ()), (YN, 1, YO, ()))
    for u in range(last + 1):
        add(True, u, (2, 1, 1) if u == last else (4,), (YN, 0, YT, (XD,)), (XN, 1, XT, (YD,)))
    for u in range(last + 1):
        add(False, u, (2, 1, 1) if u == last else (4,), (ME, 0, None, (XO, YT)), (ME, 1, None, (YO, XT)))
    return steps


def exchange_list(steps, half, units):
    first = [(s.block, s.u, s.h * half[units[s.u][0]] + s.r0, s.nr) for s in steps if s.block == DG]
    return first + [(block, u, 0, 2 * half[i]) for two in ((XN, YN), (ME,)) for u, (i, _) in enumerate(units) for block in two]


def make_order(units, half):
    pieces = []
    for u, (i, _) in enumerate(units):
        for r0, nr in cuts(half[i], (1, 3) if u == 0 else (4,)):
            pieces += [(u, 0, r0, nr), (u, 1, r0, nr)]
    return pieces


def cost(size):
    return pl.CostEstimate(flops=size * 12, bytes_accessed=size, transcendentals=0)


def place_kernel(*refs, spots, half, moves, grown):
    k = len(spots)
    pieces_in, whole_in = refs[:k], refs[k : k + moves]
    outs = refs[k + moves + grown :][: moves + 1]
    scratch = refs[k + 2 * moves + grown + 1 :]
    bufs, moved, in_s, out_s = scratch[:k], scratch[k : k + moves], scratch[-2], scratch[-1]
    _, core, owner = neighbours()
    jobs = []
    for a in range(moves):
        layers, height = whole_in[a].shape[:2]
        size = height // 4
        for layer in range(layers):
            for p in range(4):
                at = pl.ds(p * size, size)
                jobs.append((whole_in[a].at[layer, at], moved[a].at[layer, at], outs[a].at[layer, at]))
    for z in range(k):
        block, other, h, r0 = spots[z]
        start = (2 * owner(block, 1 - core if other else core) + h) * half + r0
        at = pl.ds(pl.multiple_of(start, 16), pieces_in[z].shape[1])
        jobs.append((pieces_in[z], bufs[z], outs[moves].at[:, at]))
    loads = [functools.partial(pltpu.make_async_copy, src, buf, in_s.at[j]) for j, (src, buf, _) in enumerate(jobs)]
    stores = [functools.partial(pltpu.make_async_copy, buf, dst, out_s.at[j]) for j, (_, buf, dst) in enumerate(jobs)]
    for load in loads:
        load().start()
    for load, store in zip(loads, stores, strict=True):
        load().wait()
        store().start()
    for store in stores:
        store().wait()


def place(pieces, shape, half, into=None, moves=()):
    spots, arrays = zip(*pieces)
    grown = into is not None
    size = sum(a.size * 4 for a in (*arrays, *moves))
    jobs = len(arrays) + sum(4 * a.shape[0] for a in moves)
    like = [jax.ShapeDtypeStruct(a.shape, a.dtype) for a in moves] + [jax.ShapeDtypeStruct(shape, arrays[0].dtype)]
    in_hbm = pl.BlockSpec(memory_space=pltpu.HBM)
    out = pl.pallas_call(
        functools.partial(place_kernel, spots=spots, half=half, moves=len(moves), grown=int(grown)),
        out_shape=like,
        in_specs=[in_hbm] * (len(arrays) + len(moves) + grown),
        out_specs=[in_hbm] * len(like),
        scratch_shapes=[pltpu.VMEM(a.shape, a.dtype) for a in (*arrays, *moves)] + [pltpu.SemaphoreType.DMA((jobs,))] * 2,
        input_output_aliases={len(arrays) + len(moves): len(moves)} if grown else {},
        compiler_params=pltpu.CompilerParams(vmem_limit_bytes=67043328),
        cost_estimate=cost(size),
    )(*arrays, *moves, *((into,) if grown else ()))
    return out if moves else out[0]


def fresh_kernel(*refs):
    m, v, g, factor_ref, m_new, v_new = refs[:3], refs[3:6], refs[6:9], refs[9], refs[10:13], refs[13:16]
    bufs, in_s, out_s = refs[16:25], refs[25], refs[26]
    pieces = []
    for i in range(3):
        layers, height = m[i].shape[:2]
        pieces += [(i, layer, p * (height // 2), height // 2) for layer in range(layers) for p in range(2)]

    def loads(z):
        i, layer, r0, nr = pieces[z]
        at_rows = pl.ds(r0, nr)
        return [pltpu.make_async_copy(a[i].at[layer, at_rows], bufs[3 * t + i].at[layer, at_rows], in_s.at[t, z]) for t, a in enumerate((m, v, g))]

    def stores(z):
        i, layer, r0, nr = pieces[z]
        at_rows = pl.ds(r0, nr)
        return [pltpu.make_async_copy(bufs[3 * t + i].at[layer, at_rows], a[i].at[layer, at_rows], out_s.at[t, z]) for t, a in enumerate((m_new, v_new))]

    for z in range(len(pieces)):
        for copy in loads(z):
            copy.start()
    for z, (i, layer, r0, nr) in enumerate(pieces):
        for copy in loads(z):
            copy.wait()
        mm, vv, gg = (bufs[3 * t + i].at[layer] for t in range(3))
        tile = 65536 // mm.shape[1]

        def body(r, _, mm=mm, vv=vv, gg=gg, r0=r0, tile=tile):
            at_rows = pl.ds(pl.multiple_of(r0 + r * tile, tile), tile)
            grad = gg[at_rows, :].astype(F32) * factor_ref[0:1, 0:1]
            mm[at_rows, :], vv[at_rows, :] = moments(mm[at_rows, :], vv[at_rows, :], grad)
            return 0

        lax.fori_loop(0, nr // tile, body, 0)
        for copy in stores(z):
            copy.start()
    for z in range(len(pieces)):
        for copy in stores(z):
            copy.wait()


def fresh(m, v, sums, factor):
    pieces = 2 * sum(one.shape[0] for one in m)
    size = sum(one.size * 18 for one in m)
    dma = pltpu.SemaphoreType.DMA
    any_space = pl.BlockSpec(memory_space=pltpu.HBM)
    out = pl.pallas_call(
        fresh_kernel,
        name="fresh",
        out_shape=[jax.ShapeDtypeStruct(one.shape, F32) for one in (*m, *v)],
        in_specs=[any_space] * 9 + [pl.BlockSpec(memory_space=pltpu.VMEM)],
        out_specs=[any_space] * 6,
        scratch_shapes=[pltpu.VMEM(one.shape, one.dtype) for one in (*m, *v, *sums)] + [dma((3, pieces)), dma((2, pieces))],
        compiler_params=pltpu.CompilerParams(vmem_limit_bytes=67043328),
        cost_estimate=cost(size),
    )(*m, *v, *sums, factor)
    return out[:3], out[3:]


def solution(mesh):
    n = mesh.shape["dp"]

    def step(*arrays):
        terms, weights, m, v = (arrays[i : i + 3] for i in (0, 3, 6, 9))
        layers = weights[0].shape[0]
        blocks = [(one.shape[1] // 2, one.shape[2]) for one in m]
        kinds = (blocks[0], blocks[2])
        count = float(n * sum(one.size for one in m))
        dma = pltpu.SemaphoreType.DMA
        units = [(i, layer) for i in range(3) for layer in range(layers)]
        halves = [b[0] for b in blocks]
        steps = rs_steps(units, halves)
        pieces = sum(units[piece[0]][0] < KEPT for piece in make_order(units, halves))
        swaps = max(len(exchange_list(steps, halves, units)), pieces + 6 * KEPT * layers)
        hops = max(sum(one.send for one in steps), 2 * pieces + 2 * KEPT * layers)
        any_space = pl.BlockSpec(memory_space=pl.ANY)
        half, cols = blocks[KEPT]
        tail = half // CUT
        shapes = [one.shape for one in weights[:KEPT]] + [(layers, half, cols)] * 4 + [(layers, half - tail, cols)] * 2 + [(layers, tail, cols)] * 2
        shapes += [one.shape for one in m]
        out = pl.pallas_call(
            functools.partial(kernel, n=n, layers=layers, count=count),
            name="step",
            out_shape=[jax.ShapeDtypeStruct(shape, BF) for shape in shapes] + [jax.ShapeDtypeStruct((8, 128), F32)],
            in_specs=[any_space] * 12,
            out_specs=[any_space] * (len(shapes) + 1),
            scratch_shapes=[pltpu.VMEM((4, layers, 2 * b[0], b[1]), BF) for b in blocks]
            + [pltpu.VMEM((6, layers, *b), BF) for b in blocks]
            + [pltpu.VMEM((RING, *b), BF) for b in kinds]
            + [pltpu.VMEM((size, *b), F32) for size, b in zip(FEED, kinds, strict=True)] * 2
            + [pltpu.VMEM((size, *b), BF) for size, b in zip(FEED, kinds, strict=True)]
            + [pltpu.VMEM((n + 1, 8, 128), F32), pltpu.VMEM((8, 128), F32)]
            + [dma((3,)), dma((swaps,)), dma((3,)), dma((hops,)), dma((2, RING)), dma((3, 2, max(FEED)))]
            + [dma((2,)), dma((3, KEPT)), dma((2, KEPT)), dma((3, KEPT)), dma((4, 3)), dma((2, 2)), dma((2, 2))],
            compiler_params=pltpu.CompilerParams(collective_id=0, has_side_effects=True, vmem_limit_bytes=67043328),
        )(*terms, *weights, *m, *v)
        kept, (low, high), (m_low, m_high), (low_a, high_a), (x_low_b, y_high_b) = (out[i : i + 2] for i in range(0, 10, 2))
        sums, factor = out[10:13], out[13]

        def hop(a, flip):
            return lax.ppermute(a, "dp", [(i, i ^ flip) for i in range(n)])

        barrier = lax.optimization_barrier
        x, y, mate = n // 2, n // 4, 1
        x_low_a, y_high_a = hop(low_a, x), hop(high_a, y)
        x_high, y_low = hop(high, x), hop(low, y)
        mx_b, my_b = hop(x_low_b, mate), hop(y_high_b, mate)
        new_m, new_v = fresh(m, v, sums, factor)
        x_low_a, y_high_a, new_m, new_v = barrier((x_low_a, y_high_a, new_m, new_v))
        d_low_a, d_high_a = hop(x_low_a, y), hop(y_high_a, x)
        d_low_b, d_high_b = hop(x_low_b, y), hop(y_high_b, x)
        mx_a, my_a = hop(x_low_a, mate), hop(y_high_a, mate)
        shape, b = weights[KEPT].shape, half - tail
        first = [((ME, 0, 0, 0), low), ((ME, 0, 1, 0), high), ((ME, 1, 0, 0), m_low), ((ME, 1, 1, 0), m_high)]
        first += [((XN, 0, 0, 0), x_low_a), ((YN, 0, 1, 0), y_high_a), ((XN, 0, 0, b), x_low_b), ((YN, 0, 1, b), y_high_b)]
        first += [((XN, 1, 0, b), mx_b), ((YN, 1, 1, b), my_b)]
        gate, up, down = place(first, shape, half, moves=kept)
        x_high, y_low, gate, up, down = barrier((x_high, y_low, gate, up, down))
        mx_high, my_low = hop(x_high, mate), hop(y_low, mate)
        then = [((XN, 1, 0, 0), mx_a), ((YN, 1, 1, 0), my_a), ((XN, 0, 1, 0), x_high), ((YN, 0, 0, 0), y_low)]
        down = place(then, shape, half, down)
        d_low_a, d_high_a, down = barrier((d_low_a, d_high_a, down))
        md_low_a, md_high_a = hop(d_low_a, mate), hop(d_high_a, mate)
        more = [((XN, 1, 1, 0), mx_high), ((YN, 1, 0, 0), my_low)]
        down = place(more, shape, half, down)
        late_a = [((DG, 0, 0, 0), d_low_a), ((DG, 0, 1, 0), d_high_a), ((DG, 1, 0, 0), md_low_a), ((DG, 1, 1, 0), md_high_a)]
        down = place(late_a, shape, half, down)
        d_low_b, d_high_b, down = barrier((d_low_b, d_high_b, down))
        md_low_b, md_high_b = hop(d_low_b, mate), hop(d_high_b, mate)
        late_b = [((DG, 0, 0, b), d_low_b), ((DG, 0, 1, b), d_high_b), ((DG, 1, 0, b), md_low_b), ((DG, 1, 1, b), md_high_b)]
        down = place(late_b, shape, half, down)
        return (gate, up, down, *new_m, *new_v)

    all_of, cut = P(None, None, None), P(None, "dp", None)
    return jax.shard_map(
        step,
        mesh=mesh,
        in_specs=(P(("rep", "dp"), None, None, None),) * 3 + (all_of,) * 3 + (cut,) * 6,
        out_specs=(P("rep", None, None),) * 3 + (P("rep", "dp", None),) * 6,
        check_vma=False,
    )
```

time: 677 us -> 446 us (0.66)
  waiting for transfers between devices: 570 us -> 20.2 us
  Pallas kernels: 0 us -> 415 us
  local copies, waits for them, and re-layouts: 34.1 us -> 0 us
  other arithmetic: 33.5 us -> 0 us
  blocking collectives: 22.3 us -> 0 us
  between operations: 16.8 us -> 0.78 us
  starting transfers between devices: 0.24 us -> 10.1 us
    pallas_call x0 -> x7, Pallas kernels: none -> 415 us  [the longest x1 358 us: step(): pl.pallas_call(functools.partial(kernel, n=n, layers=layers, count=count)...]
    reduce_scatter x3 -> x0, waiting for transfers between devices: 325 us -> none  [step(): lax.psum_scatter(t[0], 'dp', scatter_dimension=1, tiled=True)]
    all_gather x3 -> x0, waiting for transfers between devices: 243 us -> none  [step(): whole = [lax.all_gather(one[0], 'dp', axis=1, tiled=True) for one in new]]
    unnamed x15 -> x0, local copies, waits for them, and re-layouts: 34.1 us -> none
    convert_element_type x3 -> x0, other arithmetic: 23.7 us -> none  [adamw(): return ((w - 0.02 * step).astype(jnp.bfloat16), m, v)]
    psum x1 -> x0, blocking collectives: 22.3 us -> none  [step(): squares = lax.psum(sum((jnp.sum(g * g) for g in gradients)), 'dp')]
    ppermute x0 -> x18, waiting for transfers between devices: none -> 20.2 us  [hop(): return lax.ppermute(a, 'dp', [(i, i ^ flip) for i in range(n)])]
    ppermute x0 -> x18, starting transfers between devices: none -> 10.1 us  [hop(): return lax.ppermute(a, 'dp', [(i, i ^ flip) for i in range(n)])]
  transfers between devices with their start and end apart: 6 -> 18, of which waited for: 6 -> 6; matrix products, arithmetic and copies ran while one was open for 3% -> 0% of each run, Pallas kernels for 0% -> 12%
where the time goes in v3:
time: 446 us
  Pallas kernels  415 us (93%)
  waiting for transfers between devices  20.2 us (5%)
  starting transfers between devices  10.1 us (2%)
    pallas_call x1, Pallas kernels, step(): pl.pallas_call(functools.partial(kernel, n=n, layers=layers, count=count)...  358 us
    pallas_call x5, Pallas kernels, place(): pl.pallas_call(functools.partial(place_kernel, spots=spots, half=half, mo...  37.7 us
    ppermute x18, waiting for transfers between devices, hop(): return lax.ppermute(a, 'dp', [(i, i ^ flip) for i in range(n)])  20.2 us
    pallas_call x1, Pallas kernels, fresh(): pl.pallas_call(fresh_kernel, name='fresh', out_shape=[jax.ShapeDtypeStruc...  19.7 us
    ppermute x18, starting transfers between devices, hop(): return lax.ppermute(a, 'dp', [(i, i ^ flip) for i in range(n)])  10.1 us
  transfers between devices with their start and end apart: 18, of which 6 were waited for; matrix products, arithmetic and copies ran while one was open for 0% of the time, Pallas kernels for 12%

profile of v3, /device:TPU:0, one launch (start us, length us, event | category | flops | bytes accessed | tf_op | source)
XLA Modules:
  0.0 446.0 jit_solution(5605664789433714612)
XLA Ops:
  0.6 357.7 %step.1 = (bf16[2,1024,4096]{2,1,0:T(8,128)(2,1)}, bf16[2,1024,4096]{2,1,0:T(8,128)(2,1)}, bf16[2,256,1024]{2,1,0:T(8,128)(2,1)}, bf16[2,256,1024]{2,1,0:T(8,128...) custom-call(bf16[1,2,1024,4096]{3,2,1,0:T(8,128)(2,1)} %refs_0_.2, ...), custom_call_target="tpu_custom_call" | custom-call | tf_op jit(solution)/shard_map/step/pallas_call | solution.py:538
  358.3 0.7 collective-permute-start.2
  359.0 1.3 collective-permute-start.3
  360.4 0.7 collective-permute-start
  361.0 1.3 collective-permute-start.1
  362.4 0.0 collective-permute-start.4
  362.4 19.7 %fresh.1 = (f32[2,128,4096]{2,1,0:T(8,128)}, f32[2,128,4096]{2,1,0:T(8,128)}, f32[2,512,1024]{2,1,0:T(8,128)}, f32[2,128,4096]{2,1,0:T(8,128)}, f32[2,128,4096]{2,1,0:T(8,128)}, /*index=5*/f32[2,512,1024]{2,1,0:T(8,128)}) custom-call(f32[2,128,4096]{2,1,0:T(8,128)} %refs_0_.3, f32[2,128,4096]{2,1,0:T(8,128)} %refs_1_.3, f32[2,512,1024]{2,1,0:T(8,128)} %refs_2_.3, ...), custom_call_target="tpu_custom_call" | custom-call | flops 679477248 | bytes 56623104 | tf_op jit(solution)/shard_map/fresh/pallas_call | solution.py:504
  382.1 0.0 collective-permute-done.2.refs_4_
  382.1 0.0 collective-permute-done.3.refs_5_
  382.1 0.5 collective-permute-start.10
  382.6 0.0 collective-permute-start.5
  382.7 0.0 collective-permute-done.4.refs_8_
  382.7 0.5 collective-permute-start.11
  383.1 2.1 collective-permute-done.5.refs_9_
  385.2 0.7 collective-permute-start.8
  385.9 14.2 %collective-permute-done.refs_2_ = bf16[2,256,1024]{2,1,0:T(8,128)(2,1)} collective-permute-done((bf16[2,256,1024]{2,1,0:T(8,128)(2,1)}, bf16[2,256,1024]{2,1,0:T(8,128)(2,1)}, u32[]{:S(2)}, u32[]{:S(2)}) %collective-permute-start) | collective-permute-done | bytes 1048608 | tf_op jit(solution)/shard_map/ppermute | solution.py:558
  400.1 0.7 collective-permute-start.9
  400.8 27.2 %shard_map.187 = (bf16[2,1024,4096]{2,1,0:T(8,128)(2,1)}, bf16[2,1024,4096]{2,1,0:T(8,128)(2,1)}, bf16[2,4096,1024]{2,1,0:T(8,128)(2,1)}) custom-call(bf16[2,256,1024]{2,1,0:T(8,128)(2,1)} %get-tuple-element.52.refs_0_, bf16[2,256,1024]{2,1,0:T(8,128)(2,1)} %get-tuple-element.51.refs_1_, bf16[2,256,1024]{2,1,0:T(8,128)(2,1)} %get-tuple-element.53.refs_2_, ...), custom_call_target="tpu_custom_call" | custom-call | flops 968884224 | bytes 80740352 | tf_op jit(solution)/shard_map/pallas_call | solution.py:445
  428.0 0.0 collective-permute-done.1.refs_3_
  428.0 0.0 collective-permute-start.14
  428.0 0.0 collective-permute-done.10.refs_0_
  428.0 0.5 collective-permute-start.15
  428.5 0.0 collective-permute-done.11.refs_1_
  428.5 3.1 shard_map.188.refs_2_
  431.6 0.0 collective-permute-done.8.refs_0_
  431.6 0.0 collective-permute-done.9.refs_1_
  431.6 0.1 collective-permute-start.12
  431.7 0.5 collective-permute-start.13
  432.2 1.3 collective-permute-start.6
  433.5 0.0 collective-permute-done.14.refs_0_
  433.5 0.7 collective-permute-start.7
  434.2 0.0 collective-permute-done.15.refs_1_
  434.2 2.6 shard_map.189.refs_4_
  436.8 0.0 collective-permute-done.12.refs_2_
  436.8 0.0 collective-permute-done.13.refs_3_
  436.8 2.9 shard_map.190.refs_4_
  439.7 1.1 collective-permute-done.6.refs_0_
  440.7 1.1 collective-permute-done.7.refs_1_
  441.8 0.0 collective-permute-start.16
  441.8 0.5 collective-permute-start.17
  442.3 1.4 collective-permute-done.16.refs_2_
  443.7 0.4 collective-permute-done.17.refs_3_
  444.0 2.0 shard_map.191
Async XLA Ops:
  358.3 23.8 %collective-permute-start.2 = (bf16[2,192,1024]{2,1,0:T(8,128)(2,1)}, bf16[2,192,1024]{2,1,0:T(8,128)(2,1)}, u32[]{:S(2)}, u32[]{:S(2)}) collective-permute-start(bf16[2,192,1024]{2,1,0:T(8,128)(2,1)} %get-tuple-element.55), channel_id=1, source_target_pairs={{0,4},{1,5},{2,6},{3,7},{4,0},{5,1},{6,2},{7,3}} | collective-permute-start | bytes 2359304 | tf_op jit(solution)/shard_map/ppermute | solution.py:558
  359.0 23.1 %collective-permute-start.3 = (bf16[2,192,1024]{2,1,0:T(8,128)(2,1)}, bf16[2,192,1024]{2,1,0:T(8,128)(2,1)}, u32[]{:S(2)}, u32[]{:S(2)}) collective-permute-start(bf16[2,192,1024]{2,1,0:T(8,128)(2,1)} %get-tuple-element.56), channel_id=1, source_target_pairs={{0,2},{1,3},{2,0},{3,1},{4,6},{5,7},{6,4},{7,5}} | collective-permute-start | bytes 2359304 | tf_op jit(solution)/shard_map/ppermute | solution.py:558
  360.4 39.7 %collective-permute-start = (bf16[2,256,1024]{2,1,0:T(8,128)(2,1)}, bf16[2,256,1024]{2,1,0:T(8,128)(2,1)}, u32[]{:S(2)}, u32[]{:S(2)}) collective-permute-start(bf16[2,256,1024]{2,1,0:T(8,128)(2,1)} %get-tuple-element.51.refs_1_), channel_id=1, source_target_pairs={{0,4},{1,5},{2,6},{3,7},{4,0},{5,1},{6,2},{7,3}} | collective-permute-start | bytes 3145736 | tf_op jit(solution)/shard_map/ppermute | solution.py:558
  361.0 66.9 %collective-permute-start.1 = (bf16[2,256,1024]{2,1,0:T(8,128)(2,1)}, bf16[2,256,1024]{2,1,0:T(8,128)(2,1)}, u32[]{:S(2)}, u32[]{:S(2)}) collective-permute-start(bf16[2,256,1024]{2,1,0:T(8,128)(2,1)} %get-tuple-element.52.refs_0_), channel_id=1, source_target_pairs={{0,2},{1,3},{2,0},{3,1},{4,6},{5,7},{6,4},{7,5}} | collective-permute-start | bytes 3145736 | tf_op jit(solution)/shard_map/ppermute | solution.py:558
  362.4 20.3 %collective-permute-start.4 = (bf16[2,64,1024]{2,1,0:T(8,128)(2,1)}, bf16[2,64,1024]{2,1,0:T(8,128)(2,1)}, u32[]{:S(2)}, u32[]{:S(2)}) collective-permute-start(bf16[2,64,1024]{2,1,0:T(8,128)(2,1)} %get-tuple-element.69.refs_6_), channel_id=1, source_target_pairs={{0,1},{1,0},{2,3},{3,2},{4,5},{5,4},{6,7},{7,6}} | collective-permute-start | bytes 786440 | tf_op jit(solution)/shard_map/ppermute | solution.py:558
  382.1 45.9 %collective-permute-start.10 = (bf16[2,192,1024]{2,1,0:T(8,128)(2,1)}, bf16[2,192,1024]{2,1,0:T(8,128)(2,1)}, u32[]{:S(2)}, u32[]{:S(2)}) collective-permute-start(bf16[2,192,1024]{2,1,0:T(8,128)(2,1)} %collective-permute-done.2.refs_4_), channel_id=1, source_target_pairs={{0,1},{1,0},{2,3},{3,2},{4,5},{5,4},{6,7},{7,6}} | collective-permute-start | bytes 2359304 | tf_op jit(solution)/shard_map/ppermute | solution.py:558
  382.6 2.6 collective-permute-start.5
  382.7 45.9 %collective-permute-start.11 = (bf16[2,192,1024]{2,1,0:T(8,128)(2,1)}, bf16[2,192,1024]{2,1,0:T(8,128)(2,1)}, u32[]{:S(2)}, u32[]{:S(2)}) collective-permute-start(bf16[2,192,1024]{2,1,0:T(8,128)(2,1)} %collective-permute-done.3.refs_5_), channel_id=1, source_target_pairs={{0,1},{1,0},{2,3},{3,2},{4,5},{5,4},{6,7},{7,6}} | collective-permute-start | bytes 2359304 | tf_op jit(solution)/shard_map/ppermute | solution.py:558
  385.2 46.4 %collective-permute-start.8 = (bf16[2,192,1024]{2,1,0:T(8,128)(2,1)}, bf16[2,192,1024]{2,1,0:T(8,128)(2,1)}, u32[]{:S(2)}, u32[]{:S(2)}) collective-permute-start(bf16[2,192,1024]{2,1,0:T(8,128)(2,1)} %collective-permute-done.2.refs_4_), channel_id=1, source_target_pairs={{0,2},{1,3},{2,0},{3,1},{4,6},{5,7},{6,4},{7,5}} | collective-permute-start | bytes 2359304 | tf_op jit(solution)/shard_map/ppermute | solution.py:558
  400.1 31.5 %collective-permute-start.9 = (bf16[2,192,1024]{2,1,0:T(8,128)(2,1)}, bf16[2,192,1024]{2,1,0:T(8,128)(2,1)}, u32[]{:S(2)}, u32[]{:S(2)}) collective-permute-start(bf16[2,192,1024]{2,1,0:T(8,128)(2,1)} %collective-permute-done.3.refs_5_), channel_id=1, source_target_pairs={{0,4},{1,5},{2,6},{3,7},{4,0},{5,1},{6,2},{7,3}} | collective-permute-start | bytes 2359304 | tf_op jit(solution)/shard_map/ppermute | solution.py:558
  428.0 5.5 %collective-permute-start.14 = (bf16[2,256,1024]{2,1,0:T(8,128)(2,1)}, bf16[2,256,1024]{2,1,0:T(8,128)(2,1)}, u32[]{:S(2)}, u32[]{:S(2)}) collective-permute-start(bf16[2,256,1024]{2,1,0:T(8,128)(2,1)} %collective-permute-done.refs_2_), channel_id=1, source_target_pairs={{0,1},{1,0},{2,3},{3,2},{4,5},{5,4},{6,7},{7,6}} | collective-permute-start | bytes 3145736 | tf_op jit(solution)/shard_map/ppermute | solution.py:558
  428.0 6.2 %collective-permute-start.15 = (bf16[2,256,1024]{2,1,0:T(8,128)(2,1)}, bf16[2,256,1024]{2,1,0:T(8,128)(2,1)}, u32[]{:S(2)}, u32[]{:S(2)}) collective-permute-start(bf16[2,256,1024]{2,1,0:T(8,128)(2,1)} %collective-permute-done.1.refs_3_), channel_id=1, source_target_pairs={{0,1},{1,0},{2,3},{3,2},{4,5},{5,4},{6,7},{7,6}} | collective-permute-start | bytes 3145736 | tf_op jit(solution)/shard_map/ppermute | solution.py:558
  431.6 5.1 %collective-permute-start.12 = (bf16[2,192,1024]{2,1,0:T(8,128)(2,1)}, bf16[2,192,1024]{2,1,0:T(8,128)(2,1)}, u32[]{:S(2)}, u32[]{:S(2)}) collective-permute-start(bf16[2,192,1024]{2,1,0:T(8,128)(2,1)} %collective-permute-done.8.refs_0_), channel_id=1, source_target_pairs={{0,1},{1,0},{2,3},{3,2},{4,5},{5,4},{6,7},{7,6}} | collective-permute-start | bytes 2359304 | tf_op jit(solution)/shard_map/ppermute | solution.py:558
  431.7 5.1 %collective-permute-start.13 = (bf16[2,192,1024]{2,1,0:T(8,128)(2,1)}, bf16[2,192,1024]{2,1,0:T(8,128)(2,1)}, u32[]{:S(2)}, u32[]{:S(2)}) collective-permute-start(bf16[2,192,1024]{2,1,0:T(8,128)(2,1)} %collective-permute-done.9.refs_1_), channel_id=1, source_target_pairs={{0,1},{1,0},{2,3},{3,2},{4,5},{5,4},{6,7},{7,6}} | collective-permute-start | bytes 2359304 | tf_op jit(solution)/shard_map/ppermute | solution.py:558
  432.2 8.6 %collective-permute-start.6 = (bf16[2,64,1024]{2,1,0:T(8,128)(2,1)}, bf16[2,64,1024]{2,1,0:T(8,128)(2,1)}, u32[]{:S(2)}, u32[]{:S(2)}) collective-permute-start(bf16[2,64,1024]{2,1,0:T(8,128)(2,1)} %get-tuple-element.69.refs_6_), channel_id=1, source_target_pairs={{0,2},{1,3},{2,0},{3,1},{4,6},{5,7},{6,4},{7,5}} | collective-permute-start | bytes 786440 | tf_op jit(solution)/shard_map/ppermute | solution.py:558
  433.5 8.3 %collective-permute-start.7 = (bf16[2,64,1024]{2,1,0:T(8,128)(2,1)}, bf16[2,64,1024]{2,1,0:T(8,128)(2,1)}, u32[]{:S(2)}, u32[]{:S(2)}) collective-permute-start(bf16[2,64,1024]{2,1,0:T(8,128)(2,1)} %get-tuple-element.70.refs_7_), channel_id=1, source_target_pairs={{0,4},{1,5},{2,6},{3,7},{4,0},{5,1},{6,2},{7,3}} | collective-permute-start | bytes 786440 | tf_op jit(solution)/shard_map/ppermute | solution.py:558
  441.8 1.9 collective-permute-start.16
  441.8 2.2 collective-permute-start.17

commit v4 on v3

--- a/solution.py
+++ b/solution.py
@@ -578,12 +578,11 @@
         down = place(then, shape, half, down)
         d_low_a, d_high_a, down = barrier((d_low_a, d_high_a, down))
         md_low_a, md_high_a = hop(d_low_a, mate), hop(d_high_a, mate)
-        more = [((XN, 1, 1, 0), mx_high), ((YN, 1, 0, 0), my_low)]
+        more = [((XN, 1, 1, 0), mx_high), ((YN, 1, 0, 0), my_low), ((DG, 0, 0, 0), d_low_a), ((DG, 0, 1, 0), d_high_a)]
         down = place(more, shape, half, down)
-        late_a = [((DG, 0, 0, 0), d_low_a), ((DG, 0, 1, 0), d_high_a), ((DG, 1, 0, 0), md_low_a), ((DG, 1, 1, 0), md_high_a)]
-        down = place(late_a, shape, half, down)
         d_low_b, d_high_b, down = barrier((d_low_b, d_high_b, down))
         md_low_b, md_high_b = hop(d_low_b, mate), hop(d_high_b, mate)
+        down = place([((DG, 1, 0, 0), md_low_a), ((DG, 1, 1, 0), md_high_a)], shape, half, down)
         late_b = [((DG, 0, 0, b), d_low_b), ((DG, 0, 1, b), d_high_b), ((DG, 1, 0, b), md_low_b), ((DG, 1, 1, b), md_high_b)]
         down = place(late_b, shape, half, down)
         return (gate, up, down, *new_m, *new_v)

time: 446 us -> 447 us (level)
  transfers between devices with their start and end apart: 18 -> 18, of which waited for: 6 -> 4; matrix products, arithmetic and copies ran while one was open for 0% -> 0% of each run, Pallas kernels for 12% -> 12%
where the time goes in v4:
time: 447 us
  Pallas kernels  415 us (93%)
  waiting for transfers between devices  21.3 us (5%)
  starting transfers between devices  9.59 us (2%)
    pallas_call x1, Pallas kernels, step(): pl.pallas_call(functools.partial(kernel, n=n, layers=layers, count=count)...  358 us
    pallas_call x5, Pallas kernels, place(): pl.pallas_call(functools.partial(place_kernel, spots=spots, half=half, mo...  37.7 us
    ppermute x18, waiting for transfers between devices, hop(): return lax.ppermute(a, 'dp', [(i, i ^ flip) for i in range(n)])  21.3 us
    pallas_call x1, Pallas kernels, fresh(): pl.pallas_call(fresh_kernel, name='fresh', out_shape=[jax.ShapeDtypeStruc...  19.7 us
    ppermute x18, starting transfers between devices, hop(): return lax.ppermute(a, 'dp', [(i, i ^ flip) for i in range(n)])  9.59 us
  transfers between devices with their start and end apart: 18, of which 4 were waited for; matrix products, arithmetic and copies ran while one was open for 0% of the time, Pallas kernels for 12%

profile of v4, /device:TPU:0, one launch (start us, length us, event | category | flops | bytes accessed | tf_op | source)
XLA Modules:
  0.0 446.6 jit_solution(4710051430780348257)
XLA Ops:
  0.6 357.7 %step.1 = (bf16[2,1024,4096]{2,1,0:T(8,128)(2,1)}, bf16[2,1024,4096]{2,1,0:T(8,128)(2,1)}, bf16[2,256,1024]{2,1,0:T(8,128)(2,1)}, bf16[2,256,1024]{2,1,0:T(8,128...) custom-call(bf16[1,2,1024,4096]{3,2,1,0:T(8,128)(2,1)} %refs_0_.2, ...), custom_call_target="tpu_custom_call" | custom-call | tf_op jit(solution)/shard_map/step/pallas_call | solution.py:538
  358.3 0.7 collective-permute-start.2
  359.0 1.3 collective-permute-start.3
  360.4 0.7 collective-permute-start
  361.0 1.3 collective-permute-start.1
  362.4 19.7 %fresh.1 = (f32[2,128,4096]{2,1,0:T(8,128)}, f32[2,128,4096]{2,1,0:T(8,128)}, f32[2,512,1024]{2,1,0:T(8,128)}, f32[2,128,4096]{2,1,0:T(8,128)}, f32[2,128,4096]{2,1,0:T(8,128)}, /*index=5*/f32[2,512,1024]{2,1,0:T(8,128)}) custom-call(f32[2,128,4096]{2,1,0:T(8,128)} %refs_0_.3, f32[2,128,4096]{2,1,0:T(8,128)} %refs_1_.3, f32[2,512,1024]{2,1,0:T(8,128)} %refs_2_.3, ...), custom_call_target="tpu_custom_call" | custom-call | flops 679477248 | bytes 56623104 | tf_op jit(solution)/shard_map/fresh/pallas_call | solution.py:504
  382.1 0.0 collective-permute-done.2.refs_4_
  382.1 0.0 collective-permute-done.3.refs_5_
  382.1 0.0 collective-permute-start.12
  382.1 0.5 collective-permute-start.4
  382.6 0.0 collective-permute-start.5
  382.6 2.5 collective-permute-done.4.refs_8_
  385.1 0.7 collective-permute-start.10
  385.8 0.0 collective-permute-done.5.refs_9_
  385.8 0.0 collective-permute-start.13
  385.8 14.3 %collective-permute-done.refs_2_ = bf16[2,256,1024]{2,1,0:T(8,128)(2,1)} collective-permute-done((bf16[2,256,1024]{2,1,0:T(8,128)(2,1)}, bf16[2,256,1024]{2,1,0:T(8,128)(2,1)}, u32[]{:S(2)}, u32[]{:S(2)}) %collective-permute-start) | collective-permute-done | bytes 1048608 | tf_op jit(solution)/shard_map/ppermute | solution.py:558
  400.1 0.7 collective-permute-start.11
  400.8 27.2 %shard_map.187 = (bf16[2,1024,4096]{2,1,0:T(8,128)(2,1)}, bf16[2,1024,4096]{2,1,0:T(8,128)(2,1)}, bf16[2,4096,1024]{2,1,0:T(8,128)(2,1)}) custom-call(bf16[2,256,1024]{2,1,0:T(8,128)(2,1)} %get-tuple-element.52.refs_0_, bf16[2,256,1024]{2,1,0:T(8,128)(2,1)} %get-tuple-element.51.refs_1_, bf16[2,256,1024]{2,1,0:T(8,128)(2,1)} %get-tuple-element.53.refs_2_, ...), custom_call_target="tpu_custom_call" | custom-call | flops 968884224 | bytes 80740352 | tf_op jit(solution)/shard_map/pallas_call | solution.py:445
  428.0 0.0 collective-permute-done.1.refs_3_
  428.0 0.0 collective-permute-start.8
  428.0 0.0 collective-permute-done.12.refs_0_
  428.0 0.5 collective-permute-start.9
  428.5 0.0 collective-permute-done.13.refs_1_
  428.5 3.1 shard_map.188.refs_4_
  431.6 0.0 collective-permute-done.10.refs_2_
  431.6 0.0 collective-permute-done.11.refs_3_
  431.6 0.1 collective-permute-start.16
  431.7 0.5 collective-permute-start.17
  432.2 1.3 collective-permute-start.6
  433.5 0.0 collective-permute-done.8.refs_0_
  433.5 0.7 collective-permute-start.7
  434.2 0.0 collective-permute-done.9.refs_1_
  434.2 3.1 shard_map.189.refs_2_
  437.3 3.4 collective-permute-done.6.refs_0_
  440.7 1.1 collective-permute-done.7.refs_1_
  441.8 0.0 collective-permute-start.14
  441.8 0.5 collective-permute-start.15
  442.3 0.0 collective-permute-done.16.refs_0_
  442.3 0.0 collective-permute-done.17.refs_1_
  442.3 2.3 shard_map.190.refs_4_
  444.6 0.0 collective-permute-done.14.refs_2_
  444.6 0.0 collective-permute-done.15.refs_3_
  444.6 2.0 shard_map.191
Async XLA Ops:
  358.3 23.8 %collective-permute-start.2 = (bf16[2,192,1024]{2,1,0:T(8,128)(2,1)}, bf16[2,192,1024]{2,1,0:T(8,128)(2,1)}, u32[]{:S(2)}, u32[]{:S(2)}) collective-permute-start(bf16[2,192,1024]{2,1,0:T(8,128)(2,1)} %get-tuple-element.55), channel_id=1, source_target_pairs={{0,4},{1,5},{2,6},{3,7},{4,0},{5,1},{6,2},{7,3}} | collective-permute-start | bytes 2359304 | tf_op jit(solution)/shard_map/ppermute | solution.py:558
  359.0 23.1 %collective-permute-start.3 = (bf16[2,192,1024]{2,1,0:T(8,128)(2,1)}, bf16[2,192,1024]{2,1,0:T(8,128)(2,1)}, u32[]{:S(2)}, u32[]{:S(2)}) collective-permute-start(bf16[2,192,1024]{2,1,0:T(8,128)(2,1)} %get-tuple-element.56), channel_id=1, source_target_pairs={{0,2},{1,3},{2,0},{3,1},{4,6},{5,7},{6,4},{7,5}} | collective-permute-start | bytes 2359304 | tf_op jit(solution)/shard_map/ppermute | solution.py:558
  360.4 39.7 %collective-permute-start = (bf16[2,256,1024]{2,1,0:T(8,128)(2,1)}, bf16[2,256,1024]{2,1,0:T(8,128)(2,1)}, u32[]{:S(2)}, u32[]{:S(2)}) collective-permute-start(bf16[2,256,1024]{2,1,0:T(8,128)(2,1)} %get-tuple-element.51.refs_1_), channel_id=1, source_target_pairs={{0,4},{1,5},{2,6},{3,7},{4,0},{5,1},{6,2},{7,3}} | collective-permute-start | bytes 3145736 | tf_op jit(solution)/shard_map/ppermute | solution.py:558
  361.0 66.9 %collective-permute-start.1 = (bf16[2,256,1024]{2,1,0:T(8,128)(2,1)}, bf16[2,256,1024]{2,1,0:T(8,128)(2,1)}, u32[]{:S(2)}, u32[]{:S(2)}) collective-permute-start(bf16[2,256,1024]{2,1,0:T(8,128)(2,1)} %get-tuple-element.52.refs_0_), channel_id=1, source_target_pairs={{0,2},{1,3},{2,0},{3,1},{4,6},{5,7},{6,4},{7,5}} | collective-permute-start | bytes 3145736 | tf_op jit(solution)/shard_map/ppermute | solution.py:558
  382.1 45.9 %collective-permute-start.12 = (bf16[2,192,1024]{2,1,0:T(8,128)(2,1)}, bf16[2,192,1024]{2,1,0:T(8,128)(2,1)}, u32[]{:S(2)}, u32[]{:S(2)}) collective-permute-start(bf16[2,192,1024]{2,1,0:T(8,128)(2,1)} %collective-permute-done.2.refs_4_), channel_id=1, source_target_pairs={{0,1},{1,0},{2,3},{3,2},{4,5},{5,4},{6,7},{7,6}} | collective-permute-start | bytes 2359304 | tf_op jit(solution)/shard_map/ppermute | solution.py:558
  382.1 3.0 collective-permute-start.4
  382.6 3.2 collective-permute-start.5
  385.1 46.5 %collective-permute-start.10 = (bf16[2,192,1024]{2,1,0:T(8,128)(2,1)}, bf16[2,192,1024]{2,1,0:T(8,128)(2,1)}, u32[]{:S(2)}, u32[]{:S(2)}) collective-permute-start(bf16[2,192,1024]{2,1,0:T(8,128)(2,1)} %collective-permute-done.2.refs_4_), channel_id=1, source_target_pairs={{0,2},{1,3},{2,0},{3,1},{4,6},{5,7},{6,4},{7,5}} | collective-permute-start | bytes 2359304 | tf_op jit(solution)/shard_map/ppermute | solution.py:558
  385.8 42.7 %collective-permute-start.13 = (bf16[2,192,1024]{2,1,0:T(8,128)(2,1)}, bf16[2,192,1024]{2,1,0:T(8,128)(2,1)}, u32[]{:S(2)}, u32[]{:S(2)}) collective-permute-start(bf16[2,192,1024]{2,1,0:T(8,128)(2,1)} %collective-permute-done.3.refs_5_), channel_id=1, source_target_pairs={{0,1},{1,0},{2,3},{3,2},{4,5},{5,4},{6,7},{7,6}} | collective-permute-start | bytes 2359304 | tf_op jit(solution)/shard_map/ppermute | solution.py:558
  400.1 31.5 %collective-permute-start.11 = (bf16[2,192,1024]{2,1,0:T(8,128)(2,1)}, bf16[2,192,1024]{2,1,0:T(8,128)(2,1)}, u32[]{:S(2)}, u32[]{:S(2)}) collective-permute-start(bf16[2,192,1024]{2,1,0:T(8,128)(2,1)} %collective-permute-done.3.refs_5_), channel_id=1, source_target_pairs={{0,4},{1,5},{2,6},{3,7},{4,0},{5,1},{6,2},{7,3}} | collective-permute-start | bytes 2359304 | tf_op jit(solution)/shard_map/ppermute | solution.py:558
  428.0 5.5 %collective-permute-start.8 = (bf16[2,256,1024]{2,1,0:T(8,128)(2,1)}, bf16[2,256,1024]{2,1,0:T(8,128)(2,1)}, u32[]{:S(2)}, u32[]{:S(2)}) collective-permute-start(bf16[2,256,1024]{2,1,0:T(8,128)(2,1)} %collective-permute-done.refs_2_), channel_id=1, source_target_pairs={{0,1},{1,0},{2,3},{3,2},{4,5},{5,4},{6,7},{7,6}} | collective-permute-start | bytes 3145736 | tf_op jit(solution)/shard_map/ppermute | solution.py:558
  428.0 6.2 %collective-permute-start.9 = (bf16[2,256,1024]{2,1,0:T(8,128)(2,1)}, bf16[2,256,1024]{2,1,0:T(8,128)(2,1)}, u32[]{:S(2)}, u32[]{:S(2)}) collective-permute-start(bf16[2,256,1024]{2,1,0:T(8,128)(2,1)} %collective-permute-done.1.refs_3_), channel_id=1, source_target_pairs={{0,1},{1,0},{2,3},{3,2},{4,5},{5,4},{6,7},{7,6}} | collective-permute-start | bytes 3145736 | tf_op jit(solution)/shard_map/ppermute | solution.py:558
  431.6 10.7 %collective-permute-start.16 = (bf16[2,192,1024]{2,1,0:T(8,128)(2,1)}, bf16[2,192,1024]{2,1,0:T(8,128)(2,1)}, u32[]{:S(2)}, u32[]{:S(2)}) collective-permute-start(bf16[2,192,1024]{2,1,0:T(8,128)(2,1)} %collective-permute-done.10.refs_2_), channel_id=1, source_target_pairs={{0,1},{1,0},{2,3},{3,2},{4,5},{5,4},{6,7},{7,6}} | collective-permute-start | bytes 2359304 | tf_op jit(solution)/shard_map/ppermute | solution.py:558
  431.7 10.6 %collective-permute-start.17 = (bf16[2,192,1024]{2,1,0:T(8,128)(2,1)}, bf16[2,192,1024]{2,1,0:T(8,128)(2,1)}, u32[]{:S(2)}, u32[]{:S(2)}) collective-permute-start(bf16[2,192,1024]{2,1,0:T(8,128)(2,1)} %collective-permute-done.11.refs_3_), channel_id=1, source_target_pairs={{0,1},{1,0},{2,3},{3,2},{4,5},{5,4},{6,7},{7,6}} | collective-permute-start | bytes 2359304 | tf_op jit(solution)/shard_map/ppermute | solution.py:558
  432.2 8.6 %collective-permute-start.6 = (bf16[2,64,1024]{2,1,0:T(8,128)(2,1)}, bf16[2,64,1024]{2,1,0:T(8,128)(2,1)}, u32[]{:S(2)}, u32[]{:S(2)}) collective-permute-start(bf16[2,64,1024]{2,1,0:T(8,128)(2,1)} %get-tuple-element.69.refs_6_), channel_id=1, source_target_pairs={{0,2},{1,3},{2,0},{3,1},{4,6},{5,7},{6,4},{7,5}} | collective-permute-start | bytes 786440 | tf_op jit(solution)/shard_map/ppermute | solution.py:558
  433.5 8.3 %collective-permute-start.7 = (bf16[2,64,1024]{2,1,0:T(8,128)(2,1)}, bf16[2,64,1024]{2,1,0:T(8,128)(2,1)}, u32[]{:S(2)}, u32[]{:S(2)}) collective-permute-start(bf16[2,64,1024]{2,1,0:T(8,128)(2,1)} %get-tuple-element.70.refs_7_), channel_id=1, source_target_pairs={{0,4},{1,5},{2,6},{3,7},{4,0},{5,1},{6,2},{7,3}} | collective-permute-start | bytes 786440 | tf_op jit(solution)/shard_map/ppermute | solution.py:558
  441.8 2.8 collective-permute-start.14
  441.8 2.8 collective-permute-start.15

commit v5 on v4

--- a/solution.py
+++ b/solution.py
@@ -51,8 +51,8 @@
         )
 
     barrier = pltpu.get_barrier_semaphore()
-    for k in range(1, n):
-        pl.semaphore_signal(barrier, inc=1, device_id={"dp": (me + k) % n}, device_id_type=pl.DeviceIdType.MESH)
+    for device in (mate, xnbr, ynbr):
+        pl.semaphore_signal(barrier, inc=1, device_id={"dp": device}, device_id_type=pl.DeviceIdType.MESH)
 
     units, kind, half = geometry(land, layers)
 
@@ -144,7 +144,7 @@
 
     next_term(0)
     next_term(0)
-    pl.semaphore_wait(barrier, n - 1)
+    pl.semaphore_wait(barrier, 3)
     for _ in range(4):
         next_exchange()
     next_term(0)

time: 447 us -> 446 us (level)
  no operation moved by 1% of the time
where the time goes in v5:
time: 446 us
  Pallas kernels  414 us (93%)
  waiting for transfers between devices  20.7 us (5%)
  starting transfers between devices  10.1 us (2%)
    pallas_call x1, Pallas kernels, step(): pl.pallas_call(functools.partial(kernel, n=n, layers=layers, count=count)...  357 us
    pallas_call x5, Pallas kernels, place(): pl.pallas_call(functools.partial(place_kernel, spots=spots, half=half, mo...  37.7 us
    ppermute x18, waiting for transfers between devices, hop(): return lax.ppermute(a, 'dp', [(i, i ^ flip) for i in range(n)])  20.7 us
    pallas_call x1, Pallas kernels, fresh(): pl.pallas_call(fresh_kernel, name='fresh', out_shape=[jax.ShapeDtypeStruc...  19.7 us
    ppermute x18, starting transfers between devices, hop(): return lax.ppermute(a, 'dp', [(i, i ^ flip) for i in range(n)])  10.1 us
  transfers between devices with their start and end apart: 18, of which 4 were waited for; matrix products, arithmetic and copies ran while one was open for 0% of the time, Pallas kernels for 12%

profile of v5, /device:TPU:0, one launch (start us, length us, event | category | flops | bytes accessed | tf_op | source)
XLA Modules:
  0.0 445.8 jit_solution(15688566283893232504)
XLA Ops:
  0.6 356.8 %step.1 = (bf16[2,1024,4096]{2,1,0:T(8,128)(2,1)}, bf16[2,1024,4096]{2,1,0:T(8,128)(2,1)}, bf16[2,256,1024]{2,1,0:T(8,128)(2,1)}, bf16[2,256,1024]{2,1,0:T(8,128...) custom-call(bf16[1,2,1024,4096]{3,2,1,0:T(8,128)(2,1)} %refs_0_.2, ...), custom_call_target="tpu_custom_call" | custom-call | tf_op jit(solution)/shard_map/step/pallas_call | solution.py:538
  357.5 1.0 collective-permute-start.2
  358.5 1.1 collective-permute-start.3
  359.5 1.0 collective-permute-start
  360.5 1.1 collective-permute-start.1
  361.5 19.7 %fresh.1 = (f32[2,128,4096]{2,1,0:T(8,128)}, f32[2,128,4096]{2,1,0:T(8,128)}, f32[2,512,1024]{2,1,0:T(8,128)}, f32[2,128,4096]{2,1,0:T(8,128)}, f32[2,128,4096]{2,1,0:T(8,128)}, /*index=5*/f32[2,512,1024]{2,1,0:T(8,128)}) custom-call(f32[2,128,4096]{2,1,0:T(8,128)} %refs_0_.3, f32[2,128,4096]{2,1,0:T(8,128)} %refs_1_.3, f32[2,512,1024]{2,1,0:T(8,128)} %refs_2_.3, ...), custom_call_target="tpu_custom_call" | custom-call | flops 679477248 | bytes 56623104 | tf_op jit(solution)/shard_map/fresh/pallas_call | solution.py:504
  381.2 0.0 collective-permute-done.2.refs_4_
  381.2 0.0 collective-permute-done.3.refs_5_
  381.2 0.0 collective-permute-start.12
  381.3 0.5 collective-permute-start.4
  381.8 0.0 collective-permute-start.5
  381.8 2.5 collective-permute-done.4.refs_8_
  384.3 1.0 collective-permute-start.10
  385.2 0.0 collective-permute-done.5.refs_9_
  385.2 0.0 collective-permute-start.13
  385.2 14.0 %collective-permute-done.refs_2_ = bf16[2,256,1024]{2,1,0:T(8,128)(2,1)} collective-permute-done((bf16[2,256,1024]{2,1,0:T(8,128)(2,1)}, bf16[2,256,1024]{2,1,0:T(8,128)(2,1)}, u32[]{:S(2)}, u32[]{:S(2)}) %collective-permute-start) | collective-permute-done | bytes 1048608 | tf_op jit(solution)/shard_map/ppermute | solution.py:558
  399.3 1.0 collective-permute-start.11
  400.2 27.2 %shard_map.187 = (bf16[2,1024,4096]{2,1,0:T(8,128)(2,1)}, bf16[2,1024,4096]{2,1,0:T(8,128)(2,1)}, bf16[2,4096,1024]{2,1,0:T(8,128)(2,1)}) custom-call(bf16[2,256,1024]{2,1,0:T(8,128)(2,1)} %get-tuple-element.52.refs_0_, bf16[2,256,1024]{2,1,0:T(8,128)(2,1)} %get-tuple-element.51.refs_1_, bf16[2,256,1024]{2,1,0:T(8,128)(2,1)} %get-tuple-element.53.refs_2_, ...), custom_call_target="tpu_custom_call" | custom-call | flops 968884224 | bytes 80740352 | tf_op jit(solution)/shard_map/pallas_call | solution.py:445
  427.4 0.0 collective-permute-done.1.refs_3_
  427.4 0.0 collective-permute-start.8
  427.4 0.0 collective-permute-done.12.refs_0_
  427.5 0.5 collective-permute-start.9
  427.9 0.0 collective-permute-done.13.refs_1_
  427.9 3.1 shard_map.188.refs_4_
  431.0 0.0 collective-permute-done.10.refs_2_
  431.1 0.0 collective-permute-done.11.refs_3_
  431.1 0.1 collective-permute-start.16
  431.1 0.5 collective-permute-start.17
  431.6 1.1 collective-permute-start.6
  432.7 0.0 collective-permute-done.8.refs_0_
  432.7 1.0 collective-permute-start.7
  433.6 0.0 collective-permute-done.9.refs_1_
  433.6 3.1 shard_map.189.refs_2_
  436.8 3.4 collective-permute-done.6.refs_0_
  440.2 0.8 collective-permute-done.7.refs_1_
  441.0 0.0 collective-permute-start.14
  441.0 0.5 collective-permute-start.15
  441.5 0.0 collective-permute-done.16.refs_0_
  441.5 0.0 collective-permute-done.17.refs_1_
  441.5 2.3 shard_map.190.refs_4_
  443.8 0.0 collective-permute-done.14.refs_2_
  443.8 0.0 collective-permute-done.15.refs_3_
  443.8 2.0 shard_map.191
Async XLA Ops:
  357.5 23.8 %collective-permute-start.2 = (bf16[2,192,1024]{2,1,0:T(8,128)(2,1)}, bf16[2,192,1024]{2,1,0:T(8,128)(2,1)}, u32[]{:S(2)}, u32[]{:S(2)}) collective-permute-start(bf16[2,192,1024]{2,1,0:T(8,128)(2,1)} %get-tuple-element.55), channel_id=1, source_target_pairs={{0,4},{1,5},{2,6},{3,7},{4,0},{5,1},{6,2},{7,3}} | collective-permute-start | bytes 2359304 | tf_op jit(solution)/shard_map/ppermute | solution.py:558
  358.5 22.8 %collective-permute-start.3 = (bf16[2,192,1024]{2,1,0:T(8,128)(2,1)}, bf16[2,192,1024]{2,1,0:T(8,128)(2,1)}, u32[]{:S(2)}, u32[]{:S(2)}) collective-permute-start(bf16[2,192,1024]{2,1,0:T(8,128)(2,1)} %get-tuple-element.56), channel_id=1, source_target_pairs={{0,2},{1,3},{2,0},{3,1},{4,6},{5,7},{6,4},{7,5}} | collective-permute-start | bytes 2359304 | tf_op jit(solution)/shard_map/ppermute | solution.py:558
  359.5 39.7 %collective-permute-start = (bf16[2,256,1024]{2,1,0:T(8,128)(2,1)}, bf16[2,256,1024]{2,1,0:T(8,128)(2,1)}, u32[]{:S(2)}, u32[]{:S(2)}) collective-permute-start(bf16[2,256,1024]{2,1,0:T(8,128)(2,1)} %get-tuple-element.51.refs_1_), channel_id=1, source_target_pairs={{0,4},{1,5},{2,6},{3,7},{4,0},{5,1},{6,2},{7,3}} | collective-permute-start | bytes 3145736 | tf_op jit(solution)/shard_map/ppermute | solution.py:558
  360.5 66.9 %collective-permute-start.1 = (bf16[2,256,1024]{2,1,0:T(8,128)(2,1)}, bf16[2,256,1024]{2,1,0:T(8,128)(2,1)}, u32[]{:S(2)}, u32[]{:S(2)}) collective-permute-start(bf16[2,256,1024]{2,1,0:T(8,128)(2,1)} %get-tuple-element.52.refs_0_), channel_id=1, source_target_pairs={{0,2},{1,3},{2,0},{3,1},{4,6},{5,7},{6,4},{7,5}} | collective-permute-start | bytes 3145736 | tf_op jit(solution)/shard_map/ppermute | solution.py:558
  381.2 46.2 %collective-permute-start.12 = (bf16[2,192,1024]{2,1,0:T(8,128)(2,1)}, bf16[2,192,1024]{2,1,0:T(8,128)(2,1)}, u32[]{:S(2)}, u32[]{:S(2)}) collective-permute-start(bf16[2,192,1024]{2,1,0:T(8,128)(2,1)} %collective-permute-done.2.refs_4_), channel_id=1, source_target_pairs={{0,1},{1,0},{2,3},{3,2},{4,5},{5,4},{6,7},{7,6}} | collective-permute-start | bytes 2359304 | tf_op jit(solution)/shard_map/ppermute | solution.py:558
  381.3 3.0 collective-permute-start.4
  381.8 3.5 collective-permute-start.5
  384.3 46.8 %collective-permute-start.10 = (bf16[2,192,1024]{2,1,0:T(8,128)(2,1)}, bf16[2,192,1024]{2,1,0:T(8,128)(2,1)}, u32[]{:S(2)}, u32[]{:S(2)}) collective-permute-start(bf16[2,192,1024]{2,1,0:T(8,128)(2,1)} %collective-permute-done.2.refs_4_), channel_id=1, source_target_pairs={{0,2},{1,3},{2,0},{3,1},{4,6},{5,7},{6,4},{7,5}} | collective-permute-start | bytes 2359304 | tf_op jit(solution)/shard_map/ppermute | solution.py:558
  385.2 42.7 %collective-permute-start.13 = (bf16[2,192,1024]{2,1,0:T(8,128)(2,1)}, bf16[2,192,1024]{2,1,0:T(8,128)(2,1)}, u32[]{:S(2)}, u32[]{:S(2)}) collective-permute-start(bf16[2,192,1024]{2,1,0:T(8,128)(2,1)} %collective-permute-done.3.refs_5_), channel_id=1, source_target_pairs={{0,1},{1,0},{2,3},{3,2},{4,5},{5,4},{6,7},{7,6}} | collective-permute-start | bytes 2359304 | tf_op jit(solution)/shard_map/ppermute | solution.py:558
  399.3 31.8 %collective-permute-start.11 = (bf16[2,192,1024]{2,1,0:T(8,128)(2,1)}, bf16[2,192,1024]{2,1,0:T(8,128)(2,1)}, u32[]{:S(2)}, u32[]{:S(2)}) collective-permute-start(bf16[2,192,1024]{2,1,0:T(8,128)(2,1)} %collective-permute-done.3.refs_5_), channel_id=1, source_target_pairs={{0,4},{1,5},{2,6},{3,7},{4,0},{5,1},{6,2},{7,3}} | collective-permute-start | bytes 2359304 | tf_op jit(solution)/shard_map/ppermute | solution.py:558
  427.4 5.3 %collective-permute-start.8 = (bf16[2,256,1024]{2,1,0:T(8,128)(2,1)}, bf16[2,256,1024]{2,1,0:T(8,128)(2,1)}, u32[]{:S(2)}, u32[]{:S(2)}) collective-permute-start(bf16[2,256,1024]{2,1,0:T(8,128)(2,1)} %collective-permute-done.refs_2_), channel_id=1, source_target_pairs={{0,1},{1,0},{2,3},{3,2},{4,5},{5,4},{6,7},{7,6}} | collective-permute-start | bytes 3145736 | tf_op jit(solution)/shard_map/ppermute | solution.py:558
  427.5 6.2 %collective-permute-start.9 = (bf16[2,256,1024]{2,1,0:T(8,128)(2,1)}, bf16[2,256,1024]{2,1,0:T(8,128)(2,1)}, u32[]{:S(2)}, u32[]{:S(2)}) collective-permute-start(bf16[2,256,1024]{2,1,0:T(8,128)(2,1)} %collective-permute-done.1.refs_3_), channel_id=1, source_target_pairs={{0,1},{1,0},{2,3},{3,2},{4,5},{5,4},{6,7},{7,6}} | collective-permute-start | bytes 3145736 | tf_op jit(solution)/shard_map/ppermute | solution.py:558
  431.1 10.4 %collective-permute-start.16 = (bf16[2,192,1024]{2,1,0:T(8,128)(2,1)}, bf16[2,192,1024]{2,1,0:T(8,128)(2,1)}, u32[]{:S(2)}, u32[]{:S(2)}) collective-permute-start(bf16[2,192,1024]{2,1,0:T(8,128)(2,1)} %collective-permute-done.10.refs_2_), channel_id=1, source_target_pairs={{0,1},{1,0},{2,3},{3,2},{4,5},{5,4},{6,7},{7,6}} | collective-permute-start | bytes 2359304 | tf_op jit(solution)/shard_map/ppermute | solution.py:558
  431.1 10.3 %collective-permute-start.17 = (bf16[2,192,1024]{2,1,0:T(8,128)(2,1)}, bf16[2,192,1024]{2,1,0:T(8,128)(2,1)}, u32[]{:S(2)}, u32[]{:S(2)}) collective-permute-start(bf16[2,192,1024]{2,1,0:T(8,128)(2,1)} %collective-permute-done.11.refs_3_), channel_id=1, source_target_pairs={{0,1},{1,0},{2,3},{3,2},{4,5},{5,4},{6,7},{7,6}} | collective-permute-start | bytes 2359304 | tf_op jit(solution)/shard_map/ppermute | solution.py:558
  431.6 8.6 %collective-permute-start.6 = (bf16[2,64,1024]{2,1,0:T(8,128)(2,1)}, bf16[2,64,1024]{2,1,0:T(8,128)(2,1)}, u32[]{:S(2)}, u32[]{:S(2)}) collective-permute-start(bf16[2,64,1024]{2,1,0:T(8,128)(2,1)} %get-tuple-element.69.refs_6_), channel_id=1, source_target_pairs={{0,2},{1,3},{2,0},{3,1},{4,6},{5,7},{6,4},{7,5}} | collective-permute-start | bytes 786440 | tf_op jit(solution)/shard_map/ppermute | solution.py:558
  432.7 8.3 %collective-permute-start.7 = (bf16[2,64,1024]{2,1,0:T(8,128)(2,1)}, bf16[2,64,1024]{2,1,0:T(8,128)(2,1)}, u32[]{:S(2)}, u32[]{:S(2)}) collective-permute-start(bf16[2,64,1024]{2,1,0:T(8,128)(2,1)} %get-tuple-element.70.refs_7_), channel_id=1, source_target_pairs={{0,4},{1,5},{2,6},{3,7},{4,0},{5,1},{6,2},{7,3}} | collective-permute-start | bytes 786440 | tf_op jit(solution)/shard_map/ppermute | solution.py:558
  441.0 2.8 collective-permute-start.14
  441.0 2.8 collective-permute-start.15

commit v6 on v5

--- a/solution.py
+++ b/solution.py
@@ -377,13 +377,13 @@
             steps.extend(Step(send, block, u, h, r0, nr, stream, needs) for block, h, stream, needs in two)
 
     for u in range(last + 1):
-        add(True, u, (1, 1, 2) if u == 0 else (4,), (DG, 0, XD, ()), (DG, 1, YD, ()))
+        add(True, u, (1, 3) if u == 0 else (4,), (DG, 0, XD, ()), (DG, 1, YD, ()))
     for u in range(last + 1):
         add(True, u, (4,), (XN, 0, XO, ()), (YN, 1, YO, ()))
     for u in range(last + 1):
-        add(True, u, (2, 1, 1) if u == last else (4,), (YN, 0, YT, (XD,)), (XN, 1, XT, (YD,)))
+        add(True, u, (3, 1) if u == last else (4,), (YN, 0, YT, (XD,)), (XN, 1, XT, (YD,)))
     for u in range(last + 1):
-        add(False, u, (2, 1, 1) if u == last else (4,), (ME, 0, None, (XO, YT)), (ME, 1, None, (YO, XT)))
+        add(False, u, (3, 1) if u == last else (4,), (ME, 0, None, (XO, YT)), (ME, 1, None, (YO, XT)))
     return steps
 
 
@@ -425,13 +425,17 @@
         at = pl.ds(pl.multiple_of(start, 16), pieces_in[z].shape[1])
         jobs.append((pieces_in[z], bufs[z], outs[moves].at[:, at]))
     loads = [functools.partial(pltpu.make_async_copy, src, buf, in_s.at[j]) for j, (src, buf, _) in enumerate(jobs)]
-    stores = [functools.partial(pltpu.make_async_copy, buf, dst, out_s.at[j]) for j, (_, buf, dst) in enumerate(jobs)]
+    each = (len(jobs) - k) // moves if moves else 1
+    done = [j // each if j < len(jobs) - k else moves + j - (len(jobs) - k) for j in range(len(jobs))]
+    stores = [functools.partial(pltpu.make_async_copy, buf, dst, out_s.at[z]) for z, (_, buf, dst) in zip(done, jobs, strict=True)]
     for load in loads:
         load().start()
     for load, store in zip(loads, stores, strict=True):
         load().wait()
         store().start()
-    for store in stores:
+    for a in range(moves):
+        pltpu.make_async_copy(moved[a], outs[a], out_s.at[a]).wait()
+    for store in stores[len(jobs) - k :]:
         store().wait()
 
 
@@ -447,7 +451,7 @@
         out_shape=like,
         in_specs=[in_hbm] * (len(arrays) + len(moves) + grown),
         out_specs=[in_hbm] * len(like),
-        scratch_shapes=[pltpu.VMEM(a.shape, a.dtype) for a in (*arrays, *moves)] + [pltpu.SemaphoreType.DMA((jobs,))] * 2,
+        scratch_shapes=[pltpu.VMEM(a.shape, a.dtype) for a in (*arrays, *moves)] + [pltpu.SemaphoreType.DMA((jobs,)), pltpu.SemaphoreType.DMA((len(arrays) + len(moves),))],
         input_output_aliases={len(arrays) + len(moves): len(moves)} if grown else {},
         compiler_params=pltpu.CompilerParams(vmem_limit_bytes=67043328),
         cost_estimate=cost(size),
@@ -471,7 +475,7 @@
     def stores(z):
         i, layer, r0, nr = pieces[z]
         at_rows = pl.ds(r0, nr)
-        return [pltpu.make_async_copy(bufs[3 * t + i].at[layer, at_rows], a[i].at[layer, at_rows], out_s.at[t, z]) for t, a in enumerate((m_new, v_new))]
+        return [pltpu.make_async_copy(bufs[3 * t + i].at[layer, at_rows], a[i].at[layer, at_rows], out_s.at[t, i]) for t, a in enumerate((m_new, v_new))]
 
     for z in range(len(pieces)):
         for copy in loads(z):
@@ -491,9 +495,9 @@
         lax.fori_loop(0, nr // tile, body, 0)
         for copy in stores(z):
             copy.start()
-    for z in range(len(pieces)):
-        for copy in stores(z):
-            copy.wait()
+    for t, arrays in enumerate((m_new, v_new)):
+        for i in range(3):
+            pltpu.make_async_copy(bufs[3 * t + i], arrays[i], out_s.at[t, i]).wait()
 
 
 def fresh(m, v, sums, factor):
@@ -507,7 +511,7 @@
         out_shape=[jax.ShapeDtypeStruct(one.shape, F32) for one in (*m, *v)],
         in_specs=[any_space] * 9 + [pl.BlockSpec(memory_space=pltpu.VMEM)],
         out_specs=[any_space] * 6,
-        scratch_shapes=[pltpu.VMEM(one.shape, one.dtype) for one in (*m, *v, *sums)] + [dma((3, pieces)), dma((2, pieces))],
+        scratch_shapes=[pltpu.VMEM(one.shape, one.dtype) for one in (*m, *v, *sums)] + [dma((3, pieces)), dma((2, 3))],
         compiler_params=pltpu.CompilerParams(vmem_limit_bytes=67043328),
         cost_estimate=cost(size),
     )(*m, *v, *sums, factor)

time: 446 us -> 446 us (level)
  no operation moved by 1% of the time
where the time goes in v6:
time: 446 us
  Pallas kernels  414 us (93%)
  waiting for transfers between devices  20.9 us (5%)
  starting transfers between devices  10.1 us (2%)
    pallas_call x1, Pallas kernels, step(): pl.pallas_call(functools.partial(kernel, n=n, layers=layers, count=count)...  357 us
    pallas_call x5, Pallas kernels, place(): pl.pallas_call(functools.partial(place_kernel, spots=spots, half=half, mo...  37.5 us
    ppermute x18, waiting for transfers between devices, hop(): return lax.ppermute(a, 'dp', [(i, i ^ flip) for i in range(n)])  20.9 us
    pallas_call x1, Pallas kernels, fresh(): pl.pallas_call(fresh_kernel, name='fresh', out_shape=[jax.ShapeDtypeStruc...  19.5 us
    ppermute x18, starting transfers between devices, hop(): return lax.ppermute(a, 'dp', [(i, i ^ flip) for i in range(n)])  10.1 us
  transfers between devices with their start and end apart: 18, of which 4 were waited for; matrix products, arithmetic and copies ran while one was open for 0% of the time, Pallas kernels for 12%

profile of v6, /device:TPU:0, one launch (start us, length us, event | category | flops | bytes accessed | tf_op | source)
XLA Modules:
  0.0 445.6 jit_solution(7079292580469141830)
XLA Ops:
  0.6 356.8 %step.1 = (bf16[2,1024,4096]{2,1,0:T(8,128)(2,1)}, bf16[2,1024,4096]{2,1,0:T(8,128)(2,1)}, bf16[2,256,1024]{2,1,0:T(8,128)(2,1)}, bf16[2,256,1024]{2,1,0:T(8,128...) custom-call(bf16[1,2,1024,4096]{3,2,1,0:T(8,128)(2,1)} %refs_0_.2, ...), custom_call_target="tpu_custom_call" | custom-call | tf_op jit(solution)/shard_map/step/pallas_call | solution.py:542
  357.4 1.0 collective-permute-start.2
  358.4 1.1 collective-permute-start.3
  359.5 1.0 collective-permute-start
  360.4 1.1 collective-permute-start.1
  361.5 19.5 %fresh.1 = (f32[2,128,4096]{2,1,0:T(8,128)}, f32[2,128,4096]{2,1,0:T(8,128)}, f32[2,512,1024]{2,1,0:T(8,128)}, f32[2,128,4096]{2,1,0:T(8,128)}, f32[2,128,4096]{2,1,0:T(8,128)}, /*index=5*/f32[2,512,1024]{2,1,0:T(8,128)}) custom-call(f32[2,128,4096]{2,1,0:T(8,128)} %refs_0_.3, f32[2,128,4096]{2,1,0:T(8,128)} %refs_1_.3, f32[2,512,1024]{2,1,0:T(8,128)} %refs_2_.3, ...), custom_call_target="tpu_custom_call" | custom-call | flops 679477248 | bytes 56623104 | tf_op jit(solution)/shard_map/fresh/pallas_call | solution.py:508
  381.0 0.0 collective-permute-done.2.refs_4_
  381.0 0.0 collective-permute-done.3.refs_5_
  381.0 0.0 collective-permute-start.12
  381.1 0.5 collective-permute-start.4
  381.6 0.0 collective-permute-start.5
  381.6 2.5 collective-permute-done.4.refs_8_
  384.1 1.0 collective-permute-start.10
  385.0 0.0 collective-permute-done.5.refs_9_
  385.0 0.0 collective-permute-start.13
  385.0 14.2 %collective-permute-done.refs_2_ = bf16[2,256,1024]{2,1,0:T(8,128)(2,1)} collective-permute-done((bf16[2,256,1024]{2,1,0:T(8,128)(2,1)}, bf16[2,256,1024]{2,1,0:T(8,128)(2,1)}, u32[]{:S(2)}, u32[]{:S(2)}) %collective-permute-start) | collective-permute-done | bytes 1048608 | tf_op jit(solution)/shard_map/ppermute | solution.py:562
  399.2 1.0 collective-permute-start.11
  400.2 27.0 %shard_map.187 = (bf16[2,1024,4096]{2,1,0:T(8,128)(2,1)}, bf16[2,1024,4096]{2,1,0:T(8,128)(2,1)}, bf16[2,4096,1024]{2,1,0:T(8,128)(2,1)}) custom-call(bf16[2,256,1024]{2,1,0:T(8,128)(2,1)} %get-tuple-element.52.refs_0_, bf16[2,256,1024]{2,1,0:T(8,128)(2,1)} %get-tuple-element.51.refs_1_, bf16[2,256,1024]{2,1,0:T(8,128)(2,1)} %get-tuple-element.53.refs_2_, ...), custom_call_target="tpu_custom_call" | custom-call | flops 968884224 | bytes 80740352 | tf_op jit(solution)/shard_map/pallas_call | solution.py:449
  427.2 0.0 collective-permute-done.1.refs_3_
  427.3 0.0 collective-permute-start.8
  427.3 0.0 collective-permute-done.12.refs_0_
  427.3 0.5 collective-permute-start.9
  427.8 0.0 collective-permute-done.13.refs_1_
  427.8 3.1 shard_map.188.refs_4_
  430.9 0.0 collective-permute-done.10.refs_2_
  430.9 0.0 collective-permute-done.11.refs_3_
  430.9 0.1 collective-permute-start.16
  431.0 0.5 collective-permute-start.17
  431.4 1.1 collective-permute-start.6
  432.5 0.0 collective-permute-done.8.refs_0_
  432.5 1.0 collective-permute-start.7
  433.5 0.0 collective-permute-done.9.refs_1_
  433.5 3.1 shard_map.189.refs_2_
  436.6 3.4 collective-permute-done.6.refs_0_
  440.0 0.8 collective-permute-done.7.refs_1_
  440.8 0.0 collective-permute-start.14
  440.8 0.5 collective-permute-start.15
  441.3 0.0 collective-permute-done.16.refs_0_
  441.3 0.0 collective-permute-done.17.refs_1_
  441.3 2.3 shard_map.190.refs_4_
  443.6 0.0 collective-permute-done.14.refs_2_
  443.6 0.0 collective-permute-done.15.refs_3_
  443.7 2.0 shard_map.191
Async XLA Ops:
  357.4 23.6 %collective-permute-start.2 = (bf16[2,192,1024]{2,1,0:T(8,128)(2,1)}, bf16[2,192,1024]{2,1,0:T(8,128)(2,1)}, u32[]{:S(2)}, u32[]{:S(2)}) collective-permute-start(bf16[2,192,1024]{2,1,0:T(8,128)(2,1)} %get-tuple-element.55), channel_id=1, source_target_pairs={{0,4},{1,5},{2,6},{3,7},{4,0},{5,1},{6,2},{7,3}} | collective-permute-start | bytes 2359304 | tf_op jit(solution)/shard_map/ppermute | solution.py:562
  358.4 22.6 %collective-permute-start.3 = (bf16[2,192,1024]{2,1,0:T(8,128)(2,1)}, bf16[2,192,1024]{2,1,0:T(8,128)(2,1)}, u32[]{:S(2)}, u32[]{:S(2)}) collective-permute-start(bf16[2,192,1024]{2,1,0:T(8,128)(2,1)} %get-tuple-element.56), channel_id=1, source_target_pairs={{0,2},{1,3},{2,0},{3,1},{4,6},{5,7},{6,4},{7,5}} | collective-permute-start | bytes 2359304 | tf_op jit(solution)/shard_map/ppermute | solution.py:562
  359.5 39.7 %collective-permute-start = (bf16[2,256,1024]{2,1,0:T(8,128)(2,1)}, bf16[2,256,1024]{2,1,0:T(8,128)(2,1)}, u32[]{:S(2)}, u32[]{:S(2)}) collective-permute-start(bf16[2,256,1024]{2,1,0:T(8,128)(2,1)} %get-tuple-element.51.refs_1_), channel_id=1, source_target_pairs={{0,4},{1,5},{2,6},{3,7},{4,0},{5,1},{6,2},{7,3}} | collective-permute-start | bytes 3145736 | tf_op jit(solution)/shard_map/ppermute | solution.py:562
  360.4 66.8 %collective-permute-start.1 = (bf16[2,256,1024]{2,1,0:T(8,128)(2,1)}, bf16[2,256,1024]{2,1,0:T(8,128)(2,1)}, u32[]{:S(2)}, u32[]{:S(2)}) collective-permute-start(bf16[2,256,1024]{2,1,0:T(8,128)(2,1)} %get-tuple-element.52.refs_0_), channel_id=1, source_target_pairs={{0,2},{1,3},{2,0},{3,1},{4,6},{5,7},{6,4},{7,5}} | collective-permute-start | bytes 3145736 | tf_op jit(solution)/shard_map/ppermute | solution.py:562
  381.0 46.2 %collective-permute-start.12 = (bf16[2,192,1024]{2,1,0:T(8,128)(2,1)}, bf16[2,192,1024]{2,1,0:T(8,128)(2,1)}, u32[]{:S(2)}, u32[]{:S(2)}) collective-permute-start(bf16[2,192,1024]{2,1,0:T(8,128)(2,1)} %collective-permute-done.2.refs_4_), channel_id=1, source_target_pairs={{0,1},{1,0},{2,3},{3,2},{4,5},{5,4},{6,7},{7,6}} | collective-permute-start | bytes 2359304 | tf_op jit(solution)/shard_map/ppermute | solution.py:562
  381.1 3.0 collective-permute-start.4
  381.6 3.5 collective-permute-start.5
  384.1 46.8 %collective-permute-start.10 = (bf16[2,192,1024]{2,1,0:T(8,128)(2,1)}, bf16[2,192,1024]{2,1,0:T(8,128)(2,1)}, u32[]{:S(2)}, u32[]{:S(2)}) collective-permute-start(bf16[2,192,1024]{2,1,0:T(8,128)(2,1)} %collective-permute-done.2.refs_4_), channel_id=1, source_target_pairs={{0,2},{1,3},{2,0},{3,1},{4,6},{5,7},{6,4},{7,5}} | collective-permute-start | bytes 2359304 | tf_op jit(solution)/shard_map/ppermute | solution.py:562
  385.0 42.8 %collective-permute-start.13 = (bf16[2,192,1024]{2,1,0:T(8,128)(2,1)}, bf16[2,192,1024]{2,1,0:T(8,128)(2,1)}, u32[]{:S(2)}, u32[]{:S(2)}) collective-permute-start(bf16[2,192,1024]{2,1,0:T(8,128)(2,1)} %collective-permute-done.3.refs_5_), channel_id=1, source_target_pairs={{0,1},{1,0},{2,3},{3,2},{4,5},{5,4},{6,7},{7,6}} | collective-permute-start | bytes 2359304 | tf_op jit(solution)/shard_map/ppermute | solution.py:562
  399.2 31.7 %collective-permute-start.11 = (bf16[2,192,1024]{2,1,0:T(8,128)(2,1)}, bf16[2,192,1024]{2,1,0:T(8,128)(2,1)}, u32[]{:S(2)}, u32[]{:S(2)}) collective-permute-start(bf16[2,192,1024]{2,1,0:T(8,128)(2,1)} %collective-permute-done.3.refs_5_), channel_id=1, source_target_pairs={{0,4},{1,5},{2,6},{3,7},{4,0},{5,1},{6,2},{7,3}} | collective-permute-start | bytes 2359304 | tf_op jit(solution)/shard_map/ppermute | solution.py:562
  427.3 5.3 %collective-permute-start.8 = (bf16[2,256,1024]{2,1,0:T(8,128)(2,1)}, bf16[2,256,1024]{2,1,0:T(8,128)(2,1)}, u32[]{:S(2)}, u32[]{:S(2)}) collective-permute-start(bf16[2,256,1024]{2,1,0:T(8,128)(2,1)} %collective-permute-done.refs_2_), channel_id=1, source_target_pairs={{0,1},{1,0},{2,3},{3,2},{4,5},{5,4},{6,7},{7,6}} | collective-permute-start | bytes 3145736 | tf_op jit(solution)/shard_map/ppermute | solution.py:562
  427.3 6.2 %collective-permute-start.9 = (bf16[2,256,1024]{2,1,0:T(8,128)(2,1)}, bf16[2,256,1024]{2,1,0:T(8,128)(2,1)}, u32[]{:S(2)}, u32[]{:S(2)}) collective-permute-start(bf16[2,256,1024]{2,1,0:T(8,128)(2,1)} %collective-permute-done.1.refs_3_), channel_id=1, source_target_pairs={{0,1},{1,0},{2,3},{3,2},{4,5},{5,4},{6,7},{7,6}} | collective-permute-start | bytes 3145736 | tf_op jit(solution)/shard_map/ppermute | solution.py:562
  430.9 10.4 %collective-permute-start.16 = (bf16[2,192,1024]{2,1,0:T(8,128)(2,1)}, bf16[2,192,1024]{2,1,0:T(8,128)(2,1)}, u32[]{:S(2)}, u32[]{:S(2)}) collective-permute-start(bf16[2,192,1024]{2,1,0:T(8,128)(2,1)} %collective-permute-done.10.refs_2_), channel_id=1, source_target_pairs={{0,1},{1,0},{2,3},{3,2},{4,5},{5,4},{6,7},{7,6}} | collective-permute-start | bytes 2359304 | tf_op jit(solution)/shard_map/ppermute | solution.py:562
  431.0 10.3 %collective-permute-start.17 = (bf16[2,192,1024]{2,1,0:T(8,128)(2,1)}, bf16[2,192,1024]{2,1,0:T(8,128)(2,1)}, u32[]{:S(2)}, u32[]{:S(2)}) collective-permute-start(bf16[2,192,1024]{2,1,0:T(8,128)(2,1)} %collective-permute-done.11.refs_3_), channel_id=1, source_target_pairs={{0,1},{1,0},{2,3},{3,2},{4,5},{5,4},{6,7},{7,6}} | collective-permute-start | bytes 2359304 | tf_op jit(solution)/shard_map/ppermute | solution.py:562
  431.4 8.6 %collective-permute-start.6 = (bf16[2,64,1024]{2,1,0:T(8,128)(2,1)}, bf16[2,64,1024]{2,1,0:T(8,128)(2,1)}, u32[]{:S(2)}, u32[]{:S(2)}) collective-permute-start(bf16[2,64,1024]{2,1,0:T(8,128)(2,1)} %get-tuple-element.69.refs_6_), channel_id=1, source_target_pairs={{0,2},{1,3},{2,0},{3,1},{4,6},{5,7},{6,4},{7,5}} | collective-permute-start | bytes 786440 | tf_op jit(solution)/shard_map/ppermute | solution.py:562
  432.5 8.3 %collective-permute-start.7 = (bf16[2,64,1024]{2,1,0:T(8,128)(2,1)}, bf16[2,64,1024]{2,1,0:T(8,128)(2,1)}, u32[]{:S(2)}, u32[]{:S(2)}) collective-permute-start(bf16[2,64,1024]{2,1,0:T(8,128)(2,1)} %get-tuple-element.70.refs_7_), channel_id=1, source_target_pairs={{0,4},{1,5},{2,6},{3,7},{4,0},{5,1},{6,2},{7,3}} | collective-permute-start | bytes 786440 | tf_op jit(solution)/shard_map/ppermute | solution.py:562
  440.8 2.8 collective-permute-start.14
  440.8 2.8 collective-permute-start.15
